TPU v7x, 32 devices: a whole 2x2x4 slice. The times are simulated.
32 devices in a mesh: slab: 8 (over z, y), shot: 4 (over x, core).
Axes of the slice: x: 2, y: 2, z: 4, core: 2. Of those that a mesh axis runs over, the one named last changes fastest.
Arguments:
- velocity: float32 [8, 512, 512], P('slab'), may hold values from 1.5 to 4.5
- initial_field: float32 [4, 8, 256, 256], P('shot', 'slab'), may hold values from -6 to 6
- anchor_x: int32 [4], P('shot'), may hold values from 0 to 256
- anchor_y: int32 [4], P('shot'), may hold values from 0 to 256
- source_cell: int32 [4], P('shot'), may hold values from 0 to 65535
- receivers: int32 [4, 256], P('shot'), may hold values from 0 to 65535
Outputs:
- traces: float32 [4, 4, 256], P('shot')
- image: float32 [8, 512, 512], P('slab', 'shot')
Inputs may be any that keep to these rules, and one draw needn't show every extreme that they name: `anchor_x`: shot i's window lies inside the model. `anchor_y`: shot i's window lies inside the model.
All inputs are finite; a program needn't handle non-finite values.
Results may differ from a plain program's by a relative error of at most 0.0003.
Values sent between devices are 32-bit elements; how exact they have to be, the bound alone decides.
No kernel may reach another device: no remote copies, remote signals or barrier semaphores. Data moves between devices by JAX's collectives and lax.ppermute only.
A program may use at most 64 MiB of HBM per device.

v0:
```python
import math

import jax
import jax.numpy as jnp
from jax import lax
from jax.experimental import pallas as pl
from jax.experimental.pallas import tpu as pltpu
from jax.sharding import PartitionSpec as P


STEPS = 4


COURANT = 0.125
AMPLITUDE = 4.0

SUBLANES = 8
LANES = 128
VMEM_LIMIT = 16 * 1024 * 1024


def wavelet(instant):
    shifted = 0.8 * (instant - 1.5)
    return (1.0 - 2.0 * shifted * shifted) * math.exp(-shifted * shifted)


def with_halo(cells, sides, width):
    for axis, dim in sides:
        count = lax.axis_size(axis)
        ends = count - 1
        head = lax.slice_in_dim(cells, 0, width, axis=dim)
        tail = lax.slice_in_dim(cells, cells.shape[dim] - width, cells.shape[dim], axis=dim)
        cells = jnp.concatenate(
            [
                lax.ppermute(tail, axis, [(i, (i + 1) % count) for i in range(ends)]),
                cells,
                lax.ppermute(head, axis, [((i + 1) % count, i) for i in range(ends)]),
            ],
            axis=dim,
        )
    return cells


def propagate(speed, field, extend, source, depth_start):
    coefficient = jnp.square(COURANT * speed)
    column_count = speed.shape[3]
    depth_place = lax.broadcasted_iota(jnp.int32, speed.shape, 1) + depth_start
    row_place = lax.broadcasted_iota(jnp.int32, speed.shape, 2)
    column_place = lax.broadcasted_iota(jnp.int32, speed.shape, 3)
    source_row = (source // column_count)[:, None, None, None]
    source_column = (source % column_count)[:, None, None, None]
    struck = (depth_place == 1) & (row_place == source_row) & (column_place == source_column)
    source_term = jnp.where(struck, coefficient, jnp.float32(0.0))
    previous = field
    current = field
    energy = jnp.zeros(speed.shape, jnp.float32)
    surfaces = []
    for instant in range(STEPS):
        padded = extend(current)
        laplacian = padded[:, 2:, 1:-1, 1:-1] + padded[:, :-2, 1:-1, 1:-1]
        laplacian = laplacian + padded[:, 1:-1, 2:, 1:-1] + padded[:, 1:-1, :-2, 1:-1]
        laplacian = laplacian + padded[:, 1:-1, 1:-1, 2:] + padded[:, 1:-1, 1:-1, :-2]
        laplacian = laplacian - 6.0 * current
        advanced = 2.0 * current - previous + coefficient * laplacian
        advanced = advanced + source_term * (AMPLITUDE * wavelet(instant))
        energy = energy + advanced * advanced
        surfaces.append(advanced[:, 0])
        previous, current = (current, advanced)
    return (energy / STEPS, jnp.stack(surfaces, axis=1))


def by_depth(velocity, initial_field, anchor_x, anchor_y, source_cell, receivers):
    slab_index = lax.axis_index("slab")
    layers, width_x, width_y = velocity.shape
    shot_count = initial_field.shape[0]
    window_rows = initial_field.shape[2]
    window_cols = initial_field.shape[3]

    def cut_window(start_x, start_y):
        return lax.dynamic_slice(
            velocity, (jnp.int32(0), start_x, start_y), (layers, window_rows, window_cols)
        )

    windows = jax.vmap(cut_window)(anchor_x, anchor_y)
    depth_start = slab_index * layers

    def extend_depth(current):
        rimmed = with_halo(current, (("slab", 1),), 1)
        return jnp.pad(rimmed, ((0, 0), (0, 0), (1, 1), (1, 1)))

    energy_here, surface = propagate(windows, initial_field, extend_depth, source_cell, depth_start)
    local_rows = surface.shape[2]
    receiver_row = receivers // window_cols
    receiver_column = receivers % window_cols
    holds = (receiver_row >= 0) & (receiver_row < local_rows) & (depth_start == 0)
    flat_local = jnp.clip(receiver_row, 0, local_rows - 1) * window_cols + receiver_column
    record_count = receivers.shape[1]
    picked = jnp.take_along_axis(
        surface.reshape(shot_count, STEPS, -1),
        jnp.broadcast_to(flat_local[:, None, :], (shot_count, STEPS, record_count)),
        axis=2,
    )
    picked = jnp.where(holds[:, None, :], picked, jnp.float32(0.0))
    traces = lax.psum(picked, "slab")
    partial_image = jnp.zeros((layers, width_x, width_y), jnp.float32)
    corner = (jnp.int32(0), anchor_x[0], anchor_y[0])
    partial_image = lax.dynamic_update_slice(partial_image, energy_here[0], corner)
    summed = lax.psum_scatter(partial_image, "shot", scatter_dimension=1, tiled=True)
    return (traces, summed)


def small_vmem(name, **options):
    return dict(compiler_params=pltpu.CompilerParams(vmem_limit_bytes=VMEM_LIMIT, **options), name=name)


def strip_of(place, slabs):
    return place % 2 * (slabs // 2) + place // 2


def strip_pack(window_rows, window_cols, width_x, slabs, strip, records):
    tall = strip + 2 * STEPS

    def body(anchor_x, anchor_y, receivers, velocity, field, *rest):
        blocks, (facts, listed, speed, pressure, planes, sems) = rest[:slabs], rest[slabs:]
        mine = lax.axis_index("slab")
        top, left = anchor_x[0], anchor_y[0]
        begin = pl.multiple_of(jnp.minimum(top // SUBLANES * SUBLANES, width_x - window_rows - SUBLANES), SUBLANES)
        pltpu.make_async_copy(field.at[0, 0], pressure, sems.at[0]).start()
        for t in range(window_rows // SUBLANES + 1):
            place = window_rows if t == window_rows // SUBLANES else (begin + t * SUBLANES) % window_rows
            pltpu.make_async_copy(
                velocity.at[0, pl.ds(pl.multiple_of(begin + t * SUBLANES, SUBLANES), SUBLANES)],
                speed.at[pl.ds(pl.multiple_of(place, SUBLANES), SUBLANES)],
                sems.at[1],
            ).start()
        listing = pltpu.make_async_copy(receivers, listed, sems.at[2])
        listing.start()
        kinds = lax.broadcasted_iota(jnp.int32, facts.shape, 0)
        facts[...] = jnp.where(kinds == 0, top, left)
        pltpu.make_async_copy(field.at[0, 0], pressure, sems.at[0]).wait()
        rolled = pltpu.roll(pressure[...], left % window_cols, axis=1)
        rolled = pltpu.roll(rolled, (top + STEPS) % window_rows, axis=0)
        planes[0, :window_rows] = rolled
        planes[0, window_rows:] = rolled[: 2 * STEPS]
        pltpu.make_async_copy(velocity.at[0, : window_rows + SUBLANES], speed, sems.at[1]).wait()
        seam = pl.ds(pl.multiple_of(begin % window_rows, SUBLANES), SUBLANES)
        below = lax.broadcasted_iota(jnp.int32, (SUBLANES, 2 * window_cols), 0) < top - begin
        speed[seam] = jnp.where(below, speed[window_rows:], speed[seam])
        columns = lax.broadcasted_iota(jnp.int32, (window_rows, window_cols), 1)
        chosen = COURANT * jnp.where(
            columns >= left, speed[:window_rows, :window_cols], speed[:window_rows, window_cols:]
        )
        coefficient = pltpu.roll(chosen * chosen, STEPS, axis=0)
        planes[1, :window_rows] = coefficient
        planes[1, window_rows:] = coefficient[: 2 * STEPS]
        for k in range(slabs):
            start = pl.multiple_of(strip_of(mine ^ k, slabs) * strip, SUBLANES)
            blocks[k][:tall] = planes[0, pl.ds(start, tall), :]
            blocks[k][tall:] = planes[1, pl.ds(start, tall), :]
        listing.wait()

    hbm = pl.BlockSpec(memory_space=pltpu.HBM)
    smem = pl.BlockSpec(memory_space=pltpu.SMEM)
    vmem = pl.BlockSpec(memory_space=pltpu.VMEM)
    return pl.pallas_call(
        body,
        out_shape=[jax.ShapeDtypeStruct((2 * tall, window_cols), jnp.float32)] * slabs
        + [
            jax.ShapeDtypeStruct((SUBLANES, window_cols), jnp.int32),
            jax.ShapeDtypeStruct((1, records), jnp.int32),
        ],
        in_specs=[smem, smem] + [hbm] * 3,
        out_specs=[vmem] * (slabs + 2),
        scratch_shapes=[
            pltpu.VMEM((window_rows + SUBLANES, 2 * window_cols), jnp.float32),
            pltpu.VMEM((window_rows, window_cols), jnp.float32),
            pltpu.VMEM((2, window_rows + 2 * STEPS, window_cols), jnp.float32),
            pltpu.SemaphoreType.DMA((3,)),
        ],
        **small_vmem("strip_pack"),
    )


def strip_steps(window_rows, window_cols, slabs, strip, records, order, chunks):
    tall = strip + 2 * STEPS
    pieces = window_cols // LANES
    sizes = [len(chunk) * pieces * strip for chunk in chunks]
    heard_rows = records // LANES * STEPS

    def body(source, facts, receivers, *rest):
        blocks, outs = dict(zip(order, rest)), rest[slabs:-4]
        keeps, gives = outs[: len(chunks)], outs[len(chunks) :]
        fields, speeds, energy, surface = rest[-4:]
        mine = lax.axis_index("slab")
        core = lax.axis_index("shot") % 2
        top, left = facts[0:1], facts[1:2]
        for k in range(slabs):
            fields[0, mine ^ k] = blocks[k][:tall]
            speeds[mine ^ k] = blocks[k][tall:]
        rows = lax.broadcasted_iota(jnp.int32, (tall, window_cols), 0)
        columns = lax.broadcasted_iota(jnp.int32, (tall, window_cols), 1)
        begin = strip_of(mine, slabs) * strip - STEPS

        def local_row(row):
            return (row + top - begin + window_rows) % window_rows

        def local_column(column):
            return (column + left) % window_cols

        inside_up = rows != local_row(0)
        inside_down = rows != local_row(window_rows - 1)
        inside_left = columns != local_column(0)
        inside_right = columns != local_column(window_cols - 1)
        struck = (rows == local_row(source[0] // window_cols)) & (columns == local_column(source[0] % window_cols))
        source_term = jnp.where(struck, speeds[1], 0.0)
        for instant in range(STEPS):
            now, then = instant % 2, (instant + 1) % 2
            for level in range(slabs):
                current = fields[now, level]
                previous = fields[then if instant else now, level]
                laplacian = jnp.where(inside_up, pltpu.roll(current, 1, axis=0), 0.0)
                laplacian = laplacian + jnp.where(inside_down, pltpu.roll(current, tall - 1, axis=0), 0.0)
                laplacian = laplacian + jnp.where(inside_left, pltpu.roll(current, 1, axis=1), 0.0)
                laplacian = laplacian + jnp.where(inside_right, pltpu.roll(current, window_cols - 1, axis=1), 0.0)
                if level > 0:
                    laplacian = laplacian + fields[now, level - 1]
                if level < slabs - 1:
                    laplacian = laplacian + fields[now, level + 1]
                laplacian = laplacian - 6.0 * current
                advanced = 2.0 * current - previous + speeds[level] * laplacian
                if level == 1:
                    advanced = advanced + source_term * (AMPLITUDE * wavelet(instant))
                if level == 0:
                    surface[instant * tall : (instant + 1) * tall] = advanced
                if instant < STEPS - 1:
                    fields[then, level] = advanced
                square = advanced * advanced
                energy[level] = square if instant == 0 else energy[level] + square
        for parts, parity in ((gives, 1 - core), (keeps, core)):
            for out, chunk, size in zip(parts, chunks, sizes):
                for j, k in enumerate(chunk):
                    level = 2 * ((mine // 2) ^ k) + parity
                    for i in range(pieces):
                        at = (j * pieces + i) * strip
                        cells = energy[level, STEPS : STEPS + strip, i * LANES : (i + 1) * LANES]
                        out[at : at + strip] = cells / STEPS
                out[size : size + SUBLANES] = facts[:, :LANES].astype(jnp.float32)
        row = (receivers[...] // window_cols + top[:, :1]) % window_rows - begin
        column = (receivers[...] % window_cols + left[:, :1]) % window_cols
        row = jnp.where((row >= STEPS) & (row < STEPS + strip), row, -1)
        cells = lax.broadcasted_iota(jnp.int32, (window_cols, records), 0)
        chosen = jnp.where(cells == column, 1.0, 0.0)
        picked = jnp.dot(surface[...], chosen, precision=lax.Precision.HIGHEST, preferred_element_type=jnp.float32)
        places = lax.broadcasted_iota(jnp.int32, (tall, records), 0)
        for n in range(STEPS):
            own = jnp.where(places == row, picked[n * tall : (n + 1) * tall], 0.0)
            own = jnp.sum(own, axis=0, keepdims=True)
            for i in range(records // LANES):
                at = sizes[0] + SUBLANES + i * STEPS + n
                for out in (keeps[0], gives[0]):
                    out[at : at + 1] = own[:, i * LANES : (i + 1) * LANES]

    vmem = pl.BlockSpec(memory_space=pltpu.VMEM)
    return pl.pallas_call(
        body,
        out_shape=[
            jax.ShapeDtypeStruct((size + SUBLANES + (0 if c else heard_rows), LANES), jnp.float32)
            for c, size in enumerate(sizes)
        ]
        * 2,
        in_specs=[pl.BlockSpec(memory_space=pltpu.SMEM)] + [vmem] * (2 + slabs),
        out_specs=[vmem] * (2 * len(chunks)),
        scratch_shapes=[
            pltpu.VMEM((2, slabs, tall, window_cols), jnp.float32),
            pltpu.VMEM((slabs, tall, window_cols), jnp.float32),
            pltpu.VMEM((slabs, tall, window_cols), jnp.float32),
            pltpu.VMEM((STEPS * tall, window_cols), jnp.float32),
        ],
        **small_vmem("strip_steps"),
    )


def strip_share(window_rows, window_cols, width_y, rows_here, strip, records, count, tells):
    pieces = window_cols // LANES
    wide = width_y // LANES
    deep = count * pieces * strip
    heard_rows = records // LANES * STEPS

    def body(keep, got, *outs):
        mine, shot = lax.axis_index("slab"), lax.axis_index("shot")
        zone, side = mine // 2, mine % 2
        shares = (keep, got)
        tags = [share[deep : deep + SUBLANES].astype(jnp.int32) for share in shares]
        columns = lax.broadcasted_iota(jnp.int32, (strip, LANES), 1)
        for out, over_x in zip(outs, (1, 0)):
            to_shot = ((shot // 2) ^ over_x) * 2 + side
            rows = lax.broadcasted_iota(jnp.int32, (strip, LANES), 0) + to_shot * rows_here + zone * strip
            insides = []
            for tag in tags:
                down, along = rows - tag[0:1], columns - tag[1:2]
                tall = (down >= 0) & (down < window_rows)
                insides.append(
                    [tall & (along >= -i * LANES) & (along < window_cols - i * LANES) for i in range(wide)]
                )
            for j in range(count):
                for i in range(wide):
                    start = (j * pieces + i % pieces) * strip
                    parts = [
                        jnp.where(inside[i], share[start : start + strip], 0.0)
                        for share, inside in zip(shares, insides)
                    ]
                    at = (j * wide + i) * strip
                    out[at : at + strip] = parts[0] + parts[1]
        if tells:
            heard, told = outs[2:]
            same_core = shot % 2 == side
            heard[...] = jnp.where(same_core, keep[deep + SUBLANES :], got[deep + SUBLANES :])
            told[...] = jnp.where(same_core, got[deep + SUBLANES :], keep[deep + SUBLANES :])

    vmem = pl.BlockSpec(memory_space=pltpu.VMEM)
    sizes = [count * wide * strip] * 2 + [heard_rows] * (2 * tells)
    return pl.pallas_call(
        body,
        out_shape=[jax.ShapeDtypeStruct((size, LANES), jnp.float32) for size in sizes],
        in_specs=[vmem] * 2,
        out_specs=[vmem] * len(sizes),
        **small_vmem("strip_share"),
    )


def strip_sum(width_y, strip, records, count):
    deep = width_y // LANES * strip
    heard_rows = records // LANES * STEPS

    def body(come, own, heard_too, heard, *outs):
        for j, out in enumerate(outs):
            out[:deep] = own[j * deep : (j + 1) * deep] + come[j * deep : (j + 1) * deep]
            out[deep:] = heard[...] + heard_too[...]

    vmem = pl.BlockSpec(memory_space=pltpu.VMEM)
    return pl.pallas_call(
        body,
        out_shape=[jax.ShapeDtypeStruct((deep + heard_rows, LANES), jnp.float32)] * count,
        in_specs=[vmem] * 4,
        out_specs=[vmem] * count,
        **small_vmem("strip_sum"),
    )


def strip_place(width_y, rows_here, slabs, strip, records, order):
    wide = width_y // LANES
    pairs = slabs // 2

    def body(*rest):
        blocks, (traces, image) = dict(zip(order, rest)), rest[pairs:]
        zone = lax.axis_index("slab") // 2
        for k in range(pairs):
            start = pl.multiple_of((zone ^ k) * strip, SUBLANES)
            for i in range(wide):
                image[0, pl.ds(start, strip), i * LANES : (i + 1) * LANES] = blocks[k][i * strip : (i + 1) * strip]
        total = blocks[0][wide * strip :]
        for k in range(1, pairs):
            total = total + blocks[k][wide * strip :]
        for i in range(records // LANES):
            traces[0, :, i * LANES : (i + 1) * LANES] = total[i * STEPS : (i + 1) * STEPS]

    vmem = pl.BlockSpec(memory_space=pltpu.VMEM)
    return pl.pallas_call(
        body,
        out_shape=[
            jax.ShapeDtypeStruct((1, STEPS, records), jnp.float32),
            jax.ShapeDtypeStruct((1, rows_here, width_y), jnp.float32),
        ],
        in_specs=[vmem] * pairs,
        out_specs=[vmem] * 2,
        **small_vmem("strip_place"),
    )


def swap(array, axis, k):
    return lax.ppermute(array, axis, [(i, i ^ k) for i in range(lax.axis_size(axis))])


def far_first(count):
    return list(reversed(range(count)))


def cross(array, k):
    slabs, shots = lax.axis_size("slab"), lax.axis_size("shot")
    pairs = []
    for place in range(slabs):
        for shot in range(shots):
            side, core = place % 2, shot % 2
            to_place = ((place // 2) ^ k) * 2 + core
            to_shot = shot // 2 * 2 + side
            pairs.append((place * shots + shot, to_place * shots + to_shot))
    return lax.ppermute(array, ("slab", "shot"), pairs)


def by_strips(velocity, initial_field, anchor_x, anchor_y, source_cell, receivers):
    slabs, shots = lax.axis_size("slab"), lax.axis_size("shot")
    window_rows, window_cols = initial_field.shape[2:]
    width_y = velocity.shape[2]
    rows_here = velocity.shape[1] // shots
    strip = window_rows // slabs
    records = receivers.shape[1]
    velocity, initial_field, receivers = (
        pltpu.with_memory_space_constraint(array, pltpu.HBM) for array in (velocity, initial_field, receivers)
    )
    *packed, facts, listed = strip_pack(window_rows, window_cols, velocity.shape[1], slabs, strip, records)(
        anchor_x, anchor_y, receivers, velocity, initial_field
    )
    order = far_first(slabs)
    held = [swap(packed[k], "slab", k) if k else packed[k] for k in order]
    pairs = slabs // 2
    chunks = ((*range(pairs // 2, pairs),), (*range(pairs // 2 - 1, -1, -1),))
    zones = [k for chunk in chunks for k in chunk]
    outs = strip_steps(window_rows, window_cols, slabs, strip, records, order, chunks)(
        source_cell, facts, listed, *held
    )
    keeps, gives = outs[: len(chunks)], outs[len(chunks) :]
    gots = []
    for give in gives:
        gots.append(swap(give, "shot", 1))
    shares, notes = [], []
    for c, chunk in enumerate(chunks):
        leave, stay, *more = strip_share(
            window_rows, window_cols, width_y, rows_here, strip, records, len(chunk), c == 0
        )(keeps[c], gots[c])
        shares.append((swap(leave, "shot", 2), stay))
        notes += more
    heard, told = notes
    heard_too = swap(told, "slab", 1)
    back = []
    for chunk, (come, stay) in zip(chunks, shares):
        sums = strip_sum(width_y, strip, records, len(chunk))(come, stay, heard_too, heard)
        for part, k in zip(sums, chunk):
            back.append(cross(part, k))
    traces, image = strip_place(width_y, rows_here, slabs, strip, records, zones)(*back)
    return (traces, image)


def strips_fit(mesh, velocity, initial_field, receivers):
    slabs, shots = mesh.shape["slab"], mesh.shape["shot"]
    layers, width_x, width_y = velocity.shape
    shot_count, levels, window_rows, window_cols = initial_field.shape
    records = receivers.shape[1]
    return (
        layers == levels == slabs
        and slabs == 8
        and shot_count == shots == 4
        and width_x == 2 * window_rows
        and width_y == 2 * window_cols
        and window_rows % (slabs * SUBLANES) == 0
        and width_x // shots == window_rows // 2
        and window_rows // slabs + 2 * STEPS <= window_rows
        and window_cols % LANES == 0
        and records % (2 * LANES) == 0
        and (2 * STEPS) % SUBLANES == 0
    )


def solution(mesh):
    placed = (
        P("slab", None, None),
        P("shot", "slab", None, None),
        P("shot"),
        P("shot"),
        P("shot"),
        P("shot", None),
    )

    def whole(velocity, initial_field, anchor_x, anchor_y, source_cell, receivers):
        fit = strips_fit(mesh, velocity, initial_field, receivers)
        step = jax.shard_map(
            by_strips if fit else by_depth,
            mesh=mesh,
            in_specs=placed,
            out_specs=(P("shot", None, None), P("slab", "shot", None)),
            check_vma=False,
        )
        return step(velocity, initial_field, anchor_x, anchor_y, source_cell, receivers)

    return whole
```

profile of v0, /device:TPU:1, one launch (start us, length us, event | category | flops | bytes accessed | tf_op | source)
XLA Modules:
  0.0 47.3 jit_solution(2669385689932430985)
XLA Ops:
  1.9 1.3 %strip_pack.1 = (f32[80,256]{1,0:T(8,128)S(1)}, f32[80,256]{1,0:T(8,128)S(1)}, f32[80,256]{1,0:T(8,128)S(1)}, f32[80,256]{1,0:T(8,128)S(1)}, f32[80,256]{1,0:T(8...) custom-call(s32[1]{0:T(128)S(6)} %copy.8.anchor_x, ...), custom_call_target="tpu_custom_call" | custom-call | tf_op jit(solution)/shard_map/strip_pack/pallas_call | solution.py:410
  3.2 5.2 %collective-permute-start = (f32[80,256]{1,0:T(8,128)S(1)}, f32[80,256]{1,0:T(8,128)S(1)}, u32[]{:S(2)}, u32[]{:S(2)}) collective-permute-start(f32[80,256]{1,0:T(8,128)S(1)} %get-tuple-element.28), channel_id=1, source_target_pairs={{0,28},{4,24},{8,20},{12,16},{16,12},{20,8},{24,4},{28,0},{1,29},{... | collective-permute-start | bytes 245768 | tf_op jit(solution)/shard_map/ppermute | solution.py:381
  8.4 0.4 collective-permute-start.2
  8.8 2.0 %collective-permute-start.3 = (f32[80,256]{1,0:T(8,128)S(1)}, f32[80,256]{1,0:T(8,128)S(1)}, u32[]{:S(2)}, u32[]{:S(2)}) collective-permute-start(f32[80,256]{1,0:T(8,128)S(1)} %get-tuple-element.31), channel_id=1, source_target_pairs={{0,16},{4,20},{8,24},{12,28},{16,0},{20,4},{24,8},{28,12},{1,17},{... | collective-permute-start | bytes 245768 | tf_op jit(solution)/shard_map/ppermute | solution.py:381
  10.8 2.0 %collective-permute-start.4 = (f32[80,256]{1,0:T(8,128)S(1)}, f32[80,256]{1,0:T(8,128)S(1)}, u32[]{:S(2)}, u32[]{:S(2)}) collective-permute-start(f32[80,256]{1,0:T(8,128)S(1)} %get-tuple-element.32), channel_id=1, source_target_pairs={{0,12},{4,8},{8,4},{12,0},{16,28},{20,24},{24,20},{28,16},{1,13},{... | collective-permute-start | bytes 245768 | tf_op jit(solution)/shard_map/ppermute | solution.py:381
  12.9 0.3 collective-permute-start.5
  13.1 0.5 collective-permute-done.1.rest_1_
  14.5 5.7 %collective-permute-done.2.rest_2_ = f32[80,256]{1,0:T(8,128)S(1)} collective-permute-done((f32[80,256]{1,0:T(8,128)S(1)}, f32[80,256]{1,0:T(8,128)S(1)}, u32[]{:S(2)}, u32[]{:S(2)}) %collective-permute-start.2) | collective-permute-done | bytes 81952 | tf_op jit(solution)/shard_map/ppermute | solution.py:381
  20.2 1.8 %collective-permute-done.3.rest_3_ = f32[80,256]{1,0:T(8,128)S(1)} collective-permute-done((f32[80,256]{1,0:T(8,128)S(1)}, f32[80,256]{1,0:T(8,128)S(1)}, u32[]{:S(2)}, u32[]{:S(2)}) %collective-permute-start.3) | collective-permute-done | bytes 81952 | tf_op jit(solution)/shard_map/ppermute | solution.py:381
  22.0 1.4 %strip_steps.1 = (f32[144,128]{1,0:T(8,128)S(1)}, f32[136,128]{1,0:T(8,128)S(1)}, f32[144,128]{1,0:T(8,128)S(1)}, f32[136,128]{1,0:T(8,128)S(1)}) custom-call(s32[1]{0:T(128)S(6)} %copy.10.source, s32[8,256]{1,0:T(8,128)S(1)} %get-tuple-element.26.facts, s32[1,256]{1,0:T(1,128)S(1)} %get-tuple-element.27.receivers, ...), custom_call_target="tpu_custom_call" | custom-call | tf_op jit(solution)/shard_map/strip_steps/pallas_call | solution.py:418
  23.4 1.9 %collective-permute-start.7 = (f32[144,128]{1,0:T(8,128)S(1)}, f32[144,128]{1,0:T(8,128)S(1)}, u32[]{:S(2)}, u32[]{:S(2)}) collective-permute-start(f32[144,128]{1,0:T(8,128)S(1)} %get-tuple-element.37), channel_id=1, source_target_pairs={{0,1},{1,0},{2,3},{3,2},{4,5},{5,4},{6,7},{7,6},{8,9},{9,8},{10,11... | collective-permute-start | bytes 221192 | tf_op jit(solution)/shard_map/ppermute | solution.py:381
  25.4 1.2 %collective-permute-done.12.got = f32[136,128]{1,0:T(8,128)S(1)} collective-permute-done((f32[136,128]{1,0:T(8,128)S(1)}, f32[136,128]{1,0:T(8,128)S(1)}, u32[]{:S(2)}, u32[]{:S(2)}) %collective-permute-start.12) | collective-permute-done | bytes 69664 | tf_op jit(solution)/shard_map/ppermute | solution.py:381
  26.7 1.3 %collective-permute-start.13 = (f32[256,128]{1,0:T(8,128)S(1)}, f32[256,128]{1,0:T(8,128)S(1)}, u32[]{:S(2)}, u32[]{:S(2)}) collective-permute-start(f32[256,128]{1,0:T(8,128)S(1)} %get-tuple-element.46), channel_id=1, source_target_pairs={{0,2},{1,3},{2,0},{3,1},{4,6},{5,7},{6,4},{7,5},{8,10},{9,11},{10,... | collective-permute-start | bytes 393224 | tf_op jit(solution)/shard_map/ppermute | solution.py:381
  28.1 0.3 collective-permute-start.8
  28.4 0.5 %collective-permute-start.9 = (f32[8,128]{1,0:T(8,128)S(1)}, f32[8,128]{1,0:T(8,128)S(1)}, u32[]{:S(2)}, u32[]{:S(2)}) collective-permute-start(f32[8,128]{1,0:T(8,128)S(1)} %get-tuple-element.40), channel_id=1, source_target_pairs={{0,4},{4,0},{8,12},{12,8},{16,20},{20,16},{24,28},{28,24},{1,5},{5... | collective-permute-start | bytes 12296 | tf_op jit(solution)/shard_map/ppermute | solution.py:381
  28.9 2.2 %collective-permute-done.9.heard_too = f32[8,128]{1,0:T(8,128)S(1)} collective-permute-done((f32[8,128]{1,0:T(8,128)S(1)}, f32[8,128]{1,0:T(8,128)S(1)}, u32[]{:S(2)}, u32[]{:S(2)}) %collective-permute-start.9) | collective-permute-done | bytes 4128 | tf_op jit(solution)/shard_map/ppermute | solution.py:381
  31.1 0.5 %collective-permute-done.13.come = f32[256,128]{1,0:T(8,128)S(1)} collective-permute-done((f32[256,128]{1,0:T(8,128)S(1)}, f32[256,128]{1,0:T(8,128)S(1)}, u32[]{:S(2)}, u32[]{:S(2)}) %collective-permute-start.13) | collective-permute-done | bytes 131104 | tf_op jit(solution)/shard_map/ppermute | solution.py:381
  31.6 3.0 %collective-permute-start.14 = (f32[136,128]{1,0:T(8,128)S(1)}, f32[136,128]{1,0:T(8,128)S(1)}, u32[]{:S(2)}, u32[]{:S(2)}) collective-permute-start(f32[136,128]{1,0:T(8,128)S(1)} %get-tuple-element.48), channel_id=1, source_target_pairs={{0,8},{1,12},{2,10},{3,14},{4,9},{5,13},{6,11},{7,15},{8,0},{9,4},... | collective-permute-start | bytes 208904 | tf_op jit(solution)/shard_map/ppermute | solution.py:397
  34.7 1.9 %collective-permute-start.15 = (f32[136,128]{1,0:T(8,128)S(1)}, f32[136,128]{1,0:T(8,128)S(1)}, u32[]{:S(2)}, u32[]{:S(2)}) collective-permute-start(f32[136,128]{1,0:T(8,128)S(1)} %get-tuple-element.49), channel_id=1, source_target_pairs={{0,0},{1,4},{2,2},{3,6},{4,1},{5,5},{6,3},{7,7},{8,8},{9,12},{10,1... | collective-permute-start | bytes 208904 | tf_op jit(solution)/shard_map/ppermute | solution.py:397
  36.6 3.5 %collective-permute-start.10 = (f32[136,128]{1,0:T(8,128)S(1)}, f32[136,128]{1,0:T(8,128)S(1)}, u32[]{:S(2)}, u32[]{:S(2)}) collective-permute-start(f32[136,128]{1,0:T(8,128)S(1)} %get-tuple-element.42), channel_id=1, source_target_pairs={{0,16},{1,20},{2,18},{3,22},{4,17},{5,21},{6,19},{7,23},{8,24},{9,... | collective-permute-start | bytes 208904 | tf_op jit(solution)/shard_map/ppermute | solution.py:397
  40.2 0.5 collective-permute-start.11
  40.7 3.3 %collective-permute-done.10.rest_0_ = f32[136,128]{1,0:T(8,128)S(1)} collective-permute-done((f32[136,128]{1,0:T(8,128)S(1)}, f32[136,128]{1,0:T(8,128)S(1)}, u32[]{:S(2)}, u32[]{:S(2)}) %collective-permute-start.10) | collective-permute-done | bytes 69664 | tf_op jit(solution)/shard_map/ppermute | solution.py:397
  44.0 2.6 %collective-permute-done.11.rest_1_ = f32[136,128]{1,0:T(8,128)S(1)} collective-permute-done((f32[136,128]{1,0:T(8,128)S(1)}, f32[136,128]{1,0:T(8,128)S(1)}, u32[]{:S(2)}, u32[]{:S(2)}) %collective-permute-start.11) | collective-permute-done | bytes 69664 | tf_op jit(solution)/shard_map/ppermute | solution.py:397
  46.6 0.7 %strip_place.1 = (f32[1,4,256]{2,1,0:T(4,128)}, f32[1,128,512]{2,1,0:T(8,128)}) custom-call(f32[136,128]{1,0:T(8,128)S(1)} %collective-permute-done.10.rest_0_, f32[136,128]{1,0:T(8,128)S(1)} %collective-permute-done.11.rest_1_, f32[136,128]{1,0:T(8,128)S(1)} %collective-permute-done.14.rest_2_, f32[136,128]{1,0:T(8,128)S(1)} %collective-permute-done.15.rest_3_), custom_call_target="tpu_custom_call" | custom-call | tf_op jit(solution)/shard_map/strip_place/pallas_call | solution.py:439
  (15 shorter events, 0.6 us)
Async XLA Ops:
  3.2 9.6 %collective-permute-start = (f32[80,256]{1,0:T(8,128)S(1)}, f32[80,256]{1,0:T(8,128)S(1)}, u32[]{:S(2)}, u32[]{:S(2)}) collective-permute-start(f32[80,256]{1,0:T(8,128)S(1)} %get-tuple-element.28), channel_id=1, source_target_pairs={{0,28},{4,24},{8,20},{12,16},{16,12},{20,8},{24,4},{28,0},{1,29},{... | collective-permute-start | bytes 245768 | tf_op jit(solution)/shard_map/ppermute | solution.py:381
  8.4 5.2 %collective-permute-start.1 = (f32[80,256]{1,0:T(8,128)S(1)}, f32[80,256]{1,0:T(8,128)S(1)}, u32[]{:S(2)}, u32[]{:S(2)}) collective-permute-start(f32[80,256]{1,0:T(8,128)S(1)} %get-tuple-element.29), channel_id=1, source_target_pairs={{0,24},{4,28},{8,16},{12,20},{16,8},{20,12},{24,0},{28,4},{1,25},{... | collective-permute-start | bytes 245768 | tf_op jit(solution)/shard_map/ppermute | solution.py:381
  8.4 11.8 %collective-permute-start.2 = (f32[80,256]{1,0:T(8,128)S(1)}, f32[80,256]{1,0:T(8,128)S(1)}, u32[]{:S(2)}, u32[]{:S(2)}) collective-permute-start(f32[80,256]{1,0:T(8,128)S(1)} %get-tuple-element.30), channel_id=1, source_target_pairs={{0,20},{4,16},{8,28},{12,24},{16,4},{20,0},{24,12},{28,8},{1,21},{... | collective-permute-start | bytes 245768 | tf_op jit(solution)/shard_map/ppermute | solution.py:381
  8.8 13.2 %collective-permute-start.3 = (f32[80,256]{1,0:T(8,128)S(1)}, f32[80,256]{1,0:T(8,128)S(1)}, u32[]{:S(2)}, u32[]{:S(2)}) collective-permute-start(f32[80,256]{1,0:T(8,128)S(1)} %get-tuple-element.31), channel_id=1, source_target_pairs={{0,16},{4,20},{8,24},{12,28},{16,0},{20,4},{24,8},{28,12},{1,17},{... | collective-permute-start | bytes 245768 | tf_op jit(solution)/shard_map/ppermute | solution.py:381
  10.8 11.2 %collective-permute-start.4 = (f32[80,256]{1,0:T(8,128)S(1)}, f32[80,256]{1,0:T(8,128)S(1)}, u32[]{:S(2)}, u32[]{:S(2)}) collective-permute-start(f32[80,256]{1,0:T(8,128)S(1)} %get-tuple-element.32), channel_id=1, source_target_pairs={{0,12},{4,8},{8,4},{12,0},{16,28},{20,24},{24,20},{28,16},{1,13},{... | collective-permute-start | bytes 245768 | tf_op jit(solution)/shard_map/ppermute | solution.py:381
  12.9 9.2 %collective-permute-start.5 = (f32[80,256]{1,0:T(8,128)S(1)}, f32[80,256]{1,0:T(8,128)S(1)}, u32[]{:S(2)}, u32[]{:S(2)}) collective-permute-start(f32[80,256]{1,0:T(8,128)S(1)} %get-tuple-element.33), channel_id=1, source_target_pairs={{0,8},{4,12},{8,0},{12,4},{16,24},{20,28},{24,16},{28,20},{1,9},{5... | collective-permute-start | bytes 245768 | tf_op jit(solution)/shard_map/ppermute | solution.py:381
  13.6 8.4 %collective-permute-start.6 = (f32[80,256]{1,0:T(8,128)S(1)}, f32[80,256]{1,0:T(8,128)S(1)}, u32[]{:S(2)}, u32[]{:S(2)}) collective-permute-start(f32[80,256]{1,0:T(8,128)S(1)} %get-tuple-element.34), channel_id=1, source_target_pairs={{0,4},{4,0},{8,12},{12,8},{16,20},{20,16},{24,28},{28,24},{1,5},{5... | collective-permute-start | bytes 245768 | tf_op jit(solution)/shard_map/ppermute | solution.py:381
  23.4 4.5 %collective-permute-start.7 = (f32[144,128]{1,0:T(8,128)S(1)}, f32[144,128]{1,0:T(8,128)S(1)}, u32[]{:S(2)}, u32[]{:S(2)}) collective-permute-start(f32[144,128]{1,0:T(8,128)S(1)} %get-tuple-element.37), channel_id=1, source_target_pairs={{0,1},{1,0},{2,3},{3,2},{4,5},{5,4},{6,7},{7,6},{8,9},{9,8},{10,11... | collective-permute-start | bytes 221192 | tf_op jit(solution)/shard_map/ppermute | solution.py:381
  25.3 1.3 %collective-permute-start.12 = (f32[136,128]{1,0:T(8,128)S(1)}, f32[136,128]{1,0:T(8,128)S(1)}, u32[]{:S(2)}, u32[]{:S(2)}) collective-permute-start(f32[136,128]{1,0:T(8,128)S(1)} %get-tuple-element.45), channel_id=1, source_target_pairs={{0,1},{1,0},{2,3},{3,2},{4,5},{5,4},{6,7},{7,6},{8,9},{9,8},{10,11... | collective-permute-start | bytes 208904 | tf_op jit(solution)/shard_map/ppermute | solution.py:381
  26.7 5.0 %collective-permute-start.13 = (f32[256,128]{1,0:T(8,128)S(1)}, f32[256,128]{1,0:T(8,128)S(1)}, u32[]{:S(2)}, u32[]{:S(2)}) collective-permute-start(f32[256,128]{1,0:T(8,128)S(1)} %get-tuple-element.46), channel_id=1, source_target_pairs={{0,2},{1,3},{2,0},{3,1},{4,6},{5,7},{6,4},{7,5},{8,10},{9,11},{10,... | collective-permute-start | bytes 393224 | tf_op jit(solution)/shard_map/ppermute | solution.py:381
  28.1 8.5 %collective-permute-start.8 = (f32[256,128]{1,0:T(8,128)S(1)}, f32[256,128]{1,0:T(8,128)S(1)}, u32[]{:S(2)}, u32[]{:S(2)}) collective-permute-start(f32[256,128]{1,0:T(8,128)S(1)} %get-tuple-element.38), channel_id=1, source_target_pairs={{0,2},{1,3},{2,0},{3,1},{4,6},{5,7},{6,4},{7,5},{8,10},{9,11},{10,... | collective-permute-start | bytes 393224 | tf_op jit(solution)/shard_map/ppermute | solution.py:381
  28.4 2.8 %collective-permute-start.9 = (f32[8,128]{1,0:T(8,128)S(1)}, f32[8,128]{1,0:T(8,128)S(1)}, u32[]{:S(2)}, u32[]{:S(2)}) collective-permute-start(f32[8,128]{1,0:T(8,128)S(1)} %get-tuple-element.40), channel_id=1, source_target_pairs={{0,4},{4,0},{8,12},{12,8},{16,20},{20,16},{24,28},{28,24},{1,5},{5... | collective-permute-start | bytes 12296 | tf_op jit(solution)/shard_map/ppermute | solution.py:381
  31.6 9.0 %collective-permute-start.14 = (f32[136,128]{1,0:T(8,128)S(1)}, f32[136,128]{1,0:T(8,128)S(1)}, u32[]{:S(2)}, u32[]{:S(2)}) collective-permute-start(f32[136,128]{1,0:T(8,128)S(1)} %get-tuple-element.48), channel_id=1, source_target_pairs={{0,8},{1,12},{2,10},{3,14},{4,9},{5,13},{6,11},{7,15},{8,0},{9,4},... | collective-permute-start | bytes 208904 | tf_op jit(solution)/shard_map/ppermute | solution.py:397
  34.7 6.0 %collective-permute-start.15 = (f32[136,128]{1,0:T(8,128)S(1)}, f32[136,128]{1,0:T(8,128)S(1)}, u32[]{:S(2)}, u32[]{:S(2)}) collective-permute-start(f32[136,128]{1,0:T(8,128)S(1)} %get-tuple-element.49), channel_id=1, source_target_pairs={{0,0},{1,4},{2,2},{3,6},{4,1},{5,5},{6,3},{7,7},{8,8},{9,12},{10,1... | collective-permute-start | bytes 208904 | tf_op jit(solution)/shard_map/ppermute | solution.py:397
  36.6 7.3 %collective-permute-start.10 = (f32[136,128]{1,0:T(8,128)S(1)}, f32[136,128]{1,0:T(8,128)S(1)}, u32[]{:S(2)}, u32[]{:S(2)}) collective-permute-start(f32[136,128]{1,0:T(8,128)S(1)} %get-tuple-element.42), channel_id=1, source_target_pairs={{0,16},{1,20},{2,18},{3,22},{4,17},{5,21},{6,19},{7,23},{8,24},{9,... | collective-permute-start | bytes 208904 | tf_op jit(solution)/shard_map/ppermute | solution.py:397
  40.2 6.4 %collective-permute-start.11 = (f32[136,128]{1,0:T(8,128)S(1)}, f32[136,128]{1,0:T(8,128)S(1)}, u32[]{:S(2)}, u32[]{:S(2)}) collective-permute-start(f32[136,128]{1,0:T(8,128)S(1)} %get-tuple-element.43), channel_id=1, source_target_pairs={{0,24},{1,28},{2,26},{3,30},{4,25},{5,29},{6,27},{7,31},{8,16},{9,... | collective-permute-start | bytes 208904 | tf_op jit(solution)/shard_map/ppermute | solution.py:397
where the time goes:
time: 47.5 us; the launch traced here: 47.3 us
  starting transfers between devices  23.2 us (49%)
  waiting for transfers between devices  17.9 us (38%)
  Pallas kernels  3.68 us (8%)
  between operations  2.65 us (6%)
    ppermute x12, starting transfers between devices, swap(): lax.ppermute(array, axis, [(i, i ^ k) for i in range(lax.axis_size(axis))])  14.2 us
    ppermute x12, waiting for transfers between devices, swap(): lax.ppermute(array, axis, [(i, i ^ k) for i in range(lax.axis_size(axis))])  11.9 us
    ppermute x4, starting transfers between devices, cross(): return lax.ppermute(array, ('slab', 'shot'), pairs)  8.96 us
    ppermute x4, waiting for transfers between devices, cross(): return lax.ppermute(array, ('slab', 'shot'), pairs)  5.96 us
    pallas_call x1, Pallas kernels, by_strips(): strip_steps(window_rows, window_cols, slabs, strip, records, order, chunks)  1.39 us
    pallas_call x1, Pallas kernels, by_strips(): strip_pack(window_rows, window_cols, velocity.shape[1], slabs, strip, rec...  1.31 us
  transfers between devices with their start and end apart: 16, of which 8 were waited for; matrix products, arithmetic and copies ran while one was open for 0% of the time, Pallas kernels for 1%

commit v1 on v0

--- a/solution.py
+++ b/solution.py
@@ -207,10 +207,10 @@
         def local_column(column):
             return (column + left) % window_cols
 
-        inside_up = rows != local_row(0)
-        inside_down = rows != local_row(window_rows - 1)
-        inside_left = columns != local_column(0)
-        inside_right = columns != local_column(window_cols - 1)
+        inside_up = jnp.where(rows != local_row(0), 1.0, 0.0)
+        inside_down = jnp.where(rows != local_row(window_rows - 1), 1.0, 0.0)
+        inside_left = jnp.where(columns != local_column(0), 1.0, 0.0)
+        inside_right = jnp.where(columns != local_column(window_cols - 1), 1.0, 0.0)
         struck = (rows == local_row(source[0] // window_cols)) & (columns == local_column(source[0] % window_cols))
         source_term = jnp.where(struck, speeds[1], 0.0)
         for instant in range(STEPS):
@@ -218,10 +218,10 @@
             for level in range(slabs):
                 current = fields[now, level]
                 previous = fields[then if instant else now, level]
-                laplacian = jnp.where(inside_up, pltpu.roll(current, 1, axis=0), 0.0)
-                laplacian = laplacian + jnp.where(inside_down, pltpu.roll(current, tall - 1, axis=0), 0.0)
-                laplacian = laplacian + jnp.where(inside_left, pltpu.roll(current, 1, axis=1), 0.0)
-                laplacian = laplacian + jnp.where(inside_right, pltpu.roll(current, window_cols - 1, axis=1), 0.0)
+                laplacian = inside_up * pltpu.roll(current, 1, axis=0)
+                laplacian = laplacian + inside_down * pltpu.roll(current, tall - 1, axis=0)
+                laplacian = laplacian + inside_left * pltpu.roll(current, 1, axis=1)
+                laplacian = laplacian + inside_right * pltpu.roll(current, window_cols - 1, axis=1)
                 if level > 0:
                     laplacian = laplacian + fields[now, level - 1]
                 if level < slabs - 1:

time: 47.5 us -> 47.4 us (level)
  no operation moved by 1% of the time
where the time goes in v1:
time: 47.4 us; the launch traced here: 47.2 us
  starting transfers between devices  23.2 us (49%)
  waiting for transfers between devices  17.9 us (38%)
  Pallas kernels  3.58 us (8%)
  between operations  2.65 us (6%)
    ppermute x12, starting transfers between devices, swap(): lax.ppermute(array, axis, [(i, i ^ k) for i in range(lax.axis_size(axis))])  14.2 us
    ppermute x12, waiting for transfers between devices, swap(): lax.ppermute(array, axis, [(i, i ^ k) for i in range(lax.axis_size(axis))])  11.9 us
    ppermute x4, starting transfers between devices, cross(): return lax.ppermute(array, ('slab', 'shot'), pairs)  8.96 us
    ppermute x4, waiting for transfers between devices, cross(): return lax.ppermute(array, ('slab', 'shot'), pairs)  5.96 us
    pallas_call x1, Pallas kernels, by_strips(): strip_pack(window_rows, window_cols, velocity.shape[1], slabs, strip, rec...  1.31 us
    pallas_call x1, Pallas kernels, by_strips(): strip_steps(window_rows, window_cols, slabs, strip, records, order, chunks)  1.29 us
  transfers between devices with their start and end apart: 16, of which 8 were waited for; matrix products, arithmetic and copies ran while one was open for 0% of the time, Pallas kernels for 1%

profile of v1, /device:TPU:1, one launch (start us, length us, event | category | flops | bytes accessed | tf_op | source)
XLA Modules:
  0.0 47.2 jit_solution(814542016031611351)
XLA Ops:
  1.9 1.3 %strip_pack.1 = (f32[80,256]{1,0:T(8,128)S(1)}, f32[80,256]{1,0:T(8,128)S(1)}, f32[80,256]{1,0:T(8,128)S(1)}, f32[80,256]{1,0:T(8,128)S(1)}, f32[80,256]{1,0:T(8...) custom-call(s32[1]{0:T(128)S(6)} %copy.8.anchor_x, ...), custom_call_target="tpu_custom_call" | custom-call | tf_op jit(solution)/shard_map/strip_pack/pallas_call | solution.py:410
  3.2 5.2 %collective-permute-start = (f32[80,256]{1,0:T(8,128)S(1)}, f32[80,256]{1,0:T(8,128)S(1)}, u32[]{:S(2)}, u32[]{:S(2)}) collective-permute-start(f32[80,256]{1,0:T(8,128)S(1)} %get-tuple-element.28), channel_id=1, source_target_pairs={{0,28},{4,24},{8,20},{12,16},{16,12},{20,8},{24,4},{28,0},{1,29},{... | collective-permute-start | bytes 245768 | tf_op jit(solution)/shard_map/ppermute | solution.py:381
  8.4 0.4 collective-permute-start.2
  8.8 2.0 %collective-permute-start.3 = (f32[80,256]{1,0:T(8,128)S(1)}, f32[80,256]{1,0:T(8,128)S(1)}, u32[]{:S(2)}, u32[]{:S(2)}) collective-permute-start(f32[80,256]{1,0:T(8,128)S(1)} %get-tuple-element.31), channel_id=1, source_target_pairs={{0,16},{4,20},{8,24},{12,28},{16,0},{20,4},{24,8},{28,12},{1,17},{... | collective-permute-start | bytes 245768 | tf_op jit(solution)/shard_map/ppermute | solution.py:381
  10.8 2.0 %collective-permute-start.4 = (f32[80,256]{1,0:T(8,128)S(1)}, f32[80,256]{1,0:T(8,128)S(1)}, u32[]{:S(2)}, u32[]{:S(2)}) collective-permute-start(f32[80,256]{1,0:T(8,128)S(1)} %get-tuple-element.32), channel_id=1, source_target_pairs={{0,12},{4,8},{8,4},{12,0},{16,28},{20,24},{24,20},{28,16},{1,13},{... | collective-permute-start | bytes 245768 | tf_op jit(solution)/shard_map/ppermute | solution.py:381
  12.9 0.3 collective-permute-start.5
  13.1 0.5 collective-permute-done.1.rest_1_
  14.5 5.7 %collective-permute-done.2.rest_2_ = f32[80,256]{1,0:T(8,128)S(1)} collective-permute-done((f32[80,256]{1,0:T(8,128)S(1)}, f32[80,256]{1,0:T(8,128)S(1)}, u32[]{:S(2)}, u32[]{:S(2)}) %collective-permute-start.2) | collective-permute-done | bytes 81952 | tf_op jit(solution)/shard_map/ppermute | solution.py:381
  20.2 1.8 %collective-permute-done.3.rest_3_ = f32[80,256]{1,0:T(8,128)S(1)} collective-permute-done((f32[80,256]{1,0:T(8,128)S(1)}, f32[80,256]{1,0:T(8,128)S(1)}, u32[]{:S(2)}, u32[]{:S(2)}) %collective-permute-start.3) | collective-permute-done | bytes 81952 | tf_op jit(solution)/shard_map/ppermute | solution.py:381
  22.0 1.3 %strip_steps.1 = (f32[144,128]{1,0:T(8,128)S(1)}, f32[136,128]{1,0:T(8,128)S(1)}, f32[144,128]{1,0:T(8,128)S(1)}, f32[136,128]{1,0:T(8,128)S(1)}) custom-call(s32[1]{0:T(128)S(6)} %copy.10.source, s32[8,256]{1,0:T(8,128)S(1)} %get-tuple-element.26.facts, s32[1,256]{1,0:T(1,128)S(1)} %get-tuple-element.27.receivers, ...), custom_call_target="tpu_custom_call" | custom-call | tf_op jit(solution)/shard_map/strip_steps/pallas_call | solution.py:418
  23.3 1.9 %collective-permute-start.7 = (f32[144,128]{1,0:T(8,128)S(1)}, f32[144,128]{1,0:T(8,128)S(1)}, u32[]{:S(2)}, u32[]{:S(2)}) collective-permute-start(f32[144,128]{1,0:T(8,128)S(1)} %get-tuple-element.37), channel_id=1, source_target_pairs={{0,1},{1,0},{2,3},{3,2},{4,5},{5,4},{6,7},{7,6},{8,9},{9,8},{10,11... | collective-permute-start | bytes 221192 | tf_op jit(solution)/shard_map/ppermute | solution.py:381
  25.3 1.2 %collective-permute-done.12.got = f32[136,128]{1,0:T(8,128)S(1)} collective-permute-done((f32[136,128]{1,0:T(8,128)S(1)}, f32[136,128]{1,0:T(8,128)S(1)}, u32[]{:S(2)}, u32[]{:S(2)}) %collective-permute-start.12) | collective-permute-done | bytes 69664 | tf_op jit(solution)/shard_map/ppermute | solution.py:381
  26.6 1.3 %collective-permute-start.13 = (f32[256,128]{1,0:T(8,128)S(1)}, f32[256,128]{1,0:T(8,128)S(1)}, u32[]{:S(2)}, u32[]{:S(2)}) collective-permute-start(f32[256,128]{1,0:T(8,128)S(1)} %get-tuple-element.46), channel_id=1, source_target_pairs={{0,2},{1,3},{2,0},{3,1},{4,6},{5,7},{6,4},{7,5},{8,10},{9,11},{10,... | collective-permute-start | bytes 393224 | tf_op jit(solution)/shard_map/ppermute | solution.py:381
  28.0 0.3 collective-permute-start.8
  28.3 0.5 %collective-permute-start.9 = (f32[8,128]{1,0:T(8,128)S(1)}, f32[8,128]{1,0:T(8,128)S(1)}, u32[]{:S(2)}, u32[]{:S(2)}) collective-permute-start(f32[8,128]{1,0:T(8,128)S(1)} %get-tuple-element.40), channel_id=1, source_target_pairs={{0,4},{4,0},{8,12},{12,8},{16,20},{20,16},{24,28},{28,24},{1,5},{5... | collective-permute-start | bytes 12296 | tf_op jit(solution)/shard_map/ppermute | solution.py:381
  28.8 2.2 %collective-permute-done.9.heard_too = f32[8,128]{1,0:T(8,128)S(1)} collective-permute-done((f32[8,128]{1,0:T(8,128)S(1)}, f32[8,128]{1,0:T(8,128)S(1)}, u32[]{:S(2)}, u32[]{:S(2)}) %collective-permute-start.9) | collective-permute-done | bytes 4128 | tf_op jit(solution)/shard_map/ppermute | solution.py:381
  31.0 0.5 %collective-permute-done.13.come = f32[256,128]{1,0:T(8,128)S(1)} collective-permute-done((f32[256,128]{1,0:T(8,128)S(1)}, f32[256,128]{1,0:T(8,128)S(1)}, u32[]{:S(2)}, u32[]{:S(2)}) %collective-permute-start.13) | collective-permute-done | bytes 131104 | tf_op jit(solution)/shard_map/ppermute | solution.py:381
  31.6 3.0 %collective-permute-start.14 = (f32[136,128]{1,0:T(8,128)S(1)}, f32[136,128]{1,0:T(8,128)S(1)}, u32[]{:S(2)}, u32[]{:S(2)}) collective-permute-start(f32[136,128]{1,0:T(8,128)S(1)} %get-tuple-element.48), channel_id=1, source_target_pairs={{0,8},{1,12},{2,10},{3,14},{4,9},{5,13},{6,11},{7,15},{8,0},{9,4},... | collective-permute-start | bytes 208904 | tf_op jit(solution)/shard_map/ppermute | solution.py:397
  34.6 1.9 %collective-permute-start.15 = (f32[136,128]{1,0:T(8,128)S(1)}, f32[136,128]{1,0:T(8,128)S(1)}, u32[]{:S(2)}, u32[]{:S(2)}) collective-permute-start(f32[136,128]{1,0:T(8,128)S(1)} %get-tuple-element.49), channel_id=1, source_target_pairs={{0,0},{1,4},{2,2},{3,6},{4,1},{5,5},{6,3},{7,7},{8,8},{9,12},{10,1... | collective-permute-start | bytes 208904 | tf_op jit(solution)/shard_map/ppermute | solution.py:397
  36.5 3.5 %collective-permute-start.10 = (f32[136,128]{1,0:T(8,128)S(1)}, f32[136,128]{1,0:T(8,128)S(1)}, u32[]{:S(2)}, u32[]{:S(2)}) collective-permute-start(f32[136,128]{1,0:T(8,128)S(1)} %get-tuple-element.42), channel_id=1, source_target_pairs={{0,16},{1,20},{2,18},{3,22},{4,17},{5,21},{6,19},{7,23},{8,24},{9,... | collective-permute-start | bytes 208904 | tf_op jit(solution)/shard_map/ppermute | solution.py:397
  40.1 0.5 collective-permute-start.11
  40.6 3.3 %collective-permute-done.10.rest_0_ = f32[136,128]{1,0:T(8,128)S(1)} collective-permute-done((f32[136,128]{1,0:T(8,128)S(1)}, f32[136,128]{1,0:T(8,128)S(1)}, u32[]{:S(2)}, u32[]{:S(2)}) %collective-permute-start.10) | collective-permute-done | bytes 69664 | tf_op jit(solution)/shard_map/ppermute | solution.py:397
  43.9 2.6 %collective-permute-done.11.rest_1_ = f32[136,128]{1,0:T(8,128)S(1)} collective-permute-done((f32[136,128]{1,0:T(8,128)S(1)}, f32[136,128]{1,0:T(8,128)S(1)}, u32[]{:S(2)}, u32[]{:S(2)}) %collective-permute-start.11) | collective-permute-done | bytes 69664 | tf_op jit(solution)/shard_map/ppermute | solution.py:397
  46.5 0.7 %strip_place.1 = (f32[1,4,256]{2,1,0:T(4,128)}, f32[1,128,512]{2,1,0:T(8,128)}) custom-call(f32[136,128]{1,0:T(8,128)S(1)} %collective-permute-done.10.rest_0_, f32[136,128]{1,0:T(8,128)S(1)} %collective-permute-done.11.rest_1_, f32[136,128]{1,0:T(8,128)S(1)} %collective-permute-done.14.rest_2_, f32[136,128]{1,0:T(8,128)S(1)} %collective-permute-done.15.rest_3_), custom_call_target="tpu_custom_call" | custom-call | tf_op jit(solution)/shard_map/strip_place/pallas_call | solution.py:439
  (15 shorter events, 0.6 us)
Async XLA Ops:
  3.2 9.6 %collective-permute-start = (f32[80,256]{1,0:T(8,128)S(1)}, f32[80,256]{1,0:T(8,128)S(1)}, u32[]{:S(2)}, u32[]{:S(2)}) collective-permute-start(f32[80,256]{1,0:T(8,128)S(1)} %get-tuple-element.28), channel_id=1, source_target_pairs={{0,28},{4,24},{8,20},{12,16},{16,12},{20,8},{24,4},{28,0},{1,29},{... | collective-permute-start | bytes 245768 | tf_op jit(solution)/shard_map/ppermute | solution.py:381
  8.4 5.2 %collective-permute-start.1 = (f32[80,256]{1,0:T(8,128)S(1)}, f32[80,256]{1,0:T(8,128)S(1)}, u32[]{:S(2)}, u32[]{:S(2)}) collective-permute-start(f32[80,256]{1,0:T(8,128)S(1)} %get-tuple-element.29), channel_id=1, source_target_pairs={{0,24},{4,28},{8,16},{12,20},{16,8},{20,12},{24,0},{28,4},{1,25},{... | collective-permute-start | bytes 245768 | tf_op jit(solution)/shard_map/ppermute | solution.py:381
  8.4 11.8 %collective-permute-start.2 = (f32[80,256]{1,0:T(8,128)S(1)}, f32[80,256]{1,0:T(8,128)S(1)}, u32[]{:S(2)}, u32[]{:S(2)}) collective-permute-start(f32[80,256]{1,0:T(8,128)S(1)} %get-tuple-element.30), channel_id=1, source_target_pairs={{0,20},{4,16},{8,28},{12,24},{16,4},{20,0},{24,12},{28,8},{1,21},{... | collective-permute-start | bytes 245768 | tf_op jit(solution)/shard_map/ppermute | solution.py:381
  8.8 13.2 %collective-permute-start.3 = (f32[80,256]{1,0:T(8,128)S(1)}, f32[80,256]{1,0:T(8,128)S(1)}, u32[]{:S(2)}, u32[]{:S(2)}) collective-permute-start(f32[80,256]{1,0:T(8,128)S(1)} %get-tuple-element.31), channel_id=1, source_target_pairs={{0,16},{4,20},{8,24},{12,28},{16,0},{20,4},{24,8},{28,12},{1,17},{... | collective-permute-start | bytes 245768 | tf_op jit(solution)/shard_map/ppermute | solution.py:381
  10.8 11.2 %collective-permute-start.4 = (f32[80,256]{1,0:T(8,128)S(1)}, f32[80,256]{1,0:T(8,128)S(1)}, u32[]{:S(2)}, u32[]{:S(2)}) collective-permute-start(f32[80,256]{1,0:T(8,128)S(1)} %get-tuple-element.32), channel_id=1, source_target_pairs={{0,12},{4,8},{8,4},{12,0},{16,28},{20,24},{24,20},{28,16},{1,13},{... | collective-permute-start | bytes 245768 | tf_op jit(solution)/shard_map/ppermute | solution.py:381
  12.9 9.2 %collective-permute-start.5 = (f32[80,256]{1,0:T(8,128)S(1)}, f32[80,256]{1,0:T(8,128)S(1)}, u32[]{:S(2)}, u32[]{:S(2)}) collective-permute-start(f32[80,256]{1,0:T(8,128)S(1)} %get-tuple-element.33), channel_id=1, source_target_pairs={{0,8},{4,12},{8,0},{12,4},{16,24},{20,28},{24,16},{28,20},{1,9},{5... | collective-permute-start | bytes 245768 | tf_op jit(solution)/shard_map/ppermute | solution.py:381
  13.6 8.4 %collective-permute-start.6 = (f32[80,256]{1,0:T(8,128)S(1)}, f32[80,256]{1,0:T(8,128)S(1)}, u32[]{:S(2)}, u32[]{:S(2)}) collective-permute-start(f32[80,256]{1,0:T(8,128)S(1)} %get-tuple-element.34), channel_id=1, source_target_pairs={{0,4},{4,0},{8,12},{12,8},{16,20},{20,16},{24,28},{28,24},{1,5},{5... | collective-permute-start | bytes 245768 | tf_op jit(solution)/shard_map/ppermute | solution.py:381
  23.3 4.5 %collective-permute-start.7 = (f32[144,128]{1,0:T(8,128)S(1)}, f32[144,128]{1,0:T(8,128)S(1)}, u32[]{:S(2)}, u32[]{:S(2)}) collective-permute-start(f32[144,128]{1,0:T(8,128)S(1)} %get-tuple-element.37), channel_id=1, source_target_pairs={{0,1},{1,0},{2,3},{3,2},{4,5},{5,4},{6,7},{7,6},{8,9},{9,8},{10,11... | collective-permute-start | bytes 221192 | tf_op jit(solution)/shard_map/ppermute | solution.py:381
  25.2 1.3 %collective-permute-start.12 = (f32[136,128]{1,0:T(8,128)S(1)}, f32[136,128]{1,0:T(8,128)S(1)}, u32[]{:S(2)}, u32[]{:S(2)}) collective-permute-start(f32[136,128]{1,0:T(8,128)S(1)} %get-tuple-element.45), channel_id=1, source_target_pairs={{0,1},{1,0},{2,3},{3,2},{4,5},{5,4},{6,7},{7,6},{8,9},{9,8},{10,11... | collective-permute-start | bytes 208904 | tf_op jit(solution)/shard_map/ppermute | solution.py:381
  26.6 5.0 %collective-permute-start.13 = (f32[256,128]{1,0:T(8,128)S(1)}, f32[256,128]{1,0:T(8,128)S(1)}, u32[]{:S(2)}, u32[]{:S(2)}) collective-permute-start(f32[256,128]{1,0:T(8,128)S(1)} %get-tuple-element.46), channel_id=1, source_target_pairs={{0,2},{1,3},{2,0},{3,1},{4,6},{5,7},{6,4},{7,5},{8,10},{9,11},{10,... | collective-permute-start | bytes 393224 | tf_op jit(solution)/shard_map/ppermute | solution.py:381
  28.0 8.5 %collective-permute-start.8 = (f32[256,128]{1,0:T(8,128)S(1)}, f32[256,128]{1,0:T(8,128)S(1)}, u32[]{:S(2)}, u32[]{:S(2)}) collective-permute-start(f32[256,128]{1,0:T(8,128)S(1)} %get-tuple-element.38), channel_id=1, source_target_pairs={{0,2},{1,3},{2,0},{3,1},{4,6},{5,7},{6,4},{7,5},{8,10},{9,11},{10,... | collective-permute-start | bytes 393224 | tf_op jit(solution)/shard_map/ppermute | solution.py:381
  28.3 2.8 %collective-permute-start.9 = (f32[8,128]{1,0:T(8,128)S(1)}, f32[8,128]{1,0:T(8,128)S(1)}, u32[]{:S(2)}, u32[]{:S(2)}) collective-permute-start(f32[8,128]{1,0:T(8,128)S(1)} %get-tuple-element.40), channel_id=1, source_target_pairs={{0,4},{4,0},{8,12},{12,8},{16,20},{20,16},{24,28},{28,24},{1,5},{5... | collective-permute-start | bytes 12296 | tf_op jit(solution)/shard_map/ppermute | solution.py:381
  31.6 9.0 %collective-permute-start.14 = (f32[136,128]{1,0:T(8,128)S(1)}, f32[136,128]{1,0:T(8,128)S(1)}, u32[]{:S(2)}, u32[]{:S(2)}) collective-permute-start(f32[136,128]{1,0:T(8,128)S(1)} %get-tuple-element.48), channel_id=1, source_target_pairs={{0,8},{1,12},{2,10},{3,14},{4,9},{5,13},{6,11},{7,15},{8,0},{9,4},... | collective-permute-start | bytes 208904 | tf_op jit(solution)/shard_map/ppermute | solution.py:397
  34.6 6.0 %collective-permute-start.15 = (f32[136,128]{1,0:T(8,128)S(1)}, f32[136,128]{1,0:T(8,128)S(1)}, u32[]{:S(2)}, u32[]{:S(2)}) collective-permute-start(f32[136,128]{1,0:T(8,128)S(1)} %get-tuple-element.49), channel_id=1, source_target_pairs={{0,0},{1,4},{2,2},{3,6},{4,1},{5,5},{6,3},{7,7},{8,8},{9,12},{10,1... | collective-permute-start | bytes 208904 | tf_op jit(solution)/shard_map/ppermute | solution.py:397
  36.5 7.3 %collective-permute-start.10 = (f32[136,128]{1,0:T(8,128)S(1)}, f32[136,128]{1,0:T(8,128)S(1)}, u32[]{:S(2)}, u32[]{:S(2)}) collective-permute-start(f32[136,128]{1,0:T(8,128)S(1)} %get-tuple-element.42), channel_id=1, source_target_pairs={{0,16},{1,20},{2,18},{3,22},{4,17},{5,21},{6,19},{7,23},{8,24},{9,... | collective-permute-start | bytes 208904 | tf_op jit(solution)/shard_map/ppermute | solution.py:397
  40.1 6.4 %collective-permute-start.11 = (f32[136,128]{1,0:T(8,128)S(1)}, f32[136,128]{1,0:T(8,128)S(1)}, u32[]{:S(2)}, u32[]{:S(2)}) collective-permute-start(f32[136,128]{1,0:T(8,128)S(1)} %get-tuple-element.43), channel_id=1, source_target_pairs={{0,24},{1,28},{2,26},{3,30},{4,25},{5,29},{6,27},{7,31},{8,16},{9,... | collective-permute-start | bytes 208904 | tf_op jit(solution)/shard_map/ppermute | solution.py:397

commit v2 on v1

--- a/solution.py
+++ b/solution.py
@@ -217,7 +217,7 @@
             now, then = instant % 2, (instant + 1) % 2
             for level in range(slabs):
                 current = fields[now, level]
-                previous = fields[then if instant else now, level]
+                carried = 2.0 * current - fields[then, level] if instant else current
                 laplacian = inside_up * pltpu.roll(current, 1, axis=0)
                 laplacian = laplacian + inside_down * pltpu.roll(current, tall - 1, axis=0)
                 laplacian = laplacian + inside_left * pltpu.roll(current, 1, axis=1)
@@ -227,7 +227,7 @@
                 if level < slabs - 1:
                     laplacian = laplacian + fields[now, level + 1]
                 laplacian = laplacian - 6.0 * current
-                advanced = 2.0 * current - previous + speeds[level] * laplacian
+                advanced = carried + speeds[level] * laplacian
                 if level == 1:
                     advanced = advanced + source_term * (AMPLITUDE * wavelet(instant))
                 if level == 0:
@@ -382,7 +382,8 @@
 
 
 def far_first(count):
-    return list(reversed(range(count)))
+    half = count // 2
+    return [*range(count - 1, half, -2), *range(count - 2, half - 1, -2), *range(half - 1, -1, -1)]
 
 
 def cross(array, k):

time: 47.4 us -> 48.8 us (1.030)
  starting transfers between devices: 23.2 us -> 25.5 us
  waiting for transfers between devices: 17.9 us -> 16.9 us
    ppermute x12, starting transfers between devices: 14.2 us -> 15.8 us  [swap(): lax.ppermute(array, axis, [(i, i ^ k) for i in range(lax.axis_size(axis))])]
    ppermute x12, waiting for transfers between devices: 11.9 us -> 10.8 us  [swap(): lax.ppermute(array, axis, [(i, i ^ k) for i in range(lax.axis_size(axis))])]
    ppermute x4, starting transfers between devices: 8.96 us -> 9.67 us  [cross(): return lax.ppermute(array, ('slab', 'shot'), pairs)]
where the time goes in v2:
time: 48.8 us; the launch traced here: 48.6 us
  starting transfers between devices  25.5 us (52%)
  waiting for transfers between devices  16.9 us (35%)
  Pallas kernels  3.56 us (7%)
  between operations  2.65 us (5%)
    ppermute x12, starting transfers between devices, swap(): lax.ppermute(array, axis, [(i, i ^ k) for i in range(lax.axis_size(axis))])  15.8 us
    ppermute x12, waiting for transfers between devices, swap(): lax.ppermute(array, axis, [(i, i ^ k) for i in range(lax.axis_size(axis))])  10.8 us
    ppermute x4, starting transfers between devices, cross(): return lax.ppermute(array, ('slab', 'shot'), pairs)  9.67 us
    ppermute x4, waiting for transfers between devices, cross(): return lax.ppermute(array, ('slab', 'shot'), pairs)  6.05 us
    pallas_call x1, Pallas kernels, by_strips(): strip_pack(window_rows, window_cols, velocity.shape[1], slabs, strip, rec...  1.31 us
    pallas_call x1, Pallas kernels, by_strips(): strip_steps(window_rows, window_cols, slabs, strip, records, order, chunks)  1.27 us
  transfers between devices with their start and end apart: 16, of which 8 were waited for; matrix products, arithmetic and copies ran while one was open for 0% of the time, Pallas kernels for 1%

profile of v2, /device:TPU:1, one launch (start us, length us, event | category | flops | bytes accessed | tf_op | source)
XLA Modules:
  0.0 48.6 jit_solution(13884185826045432944)
XLA Ops:
  1.9 1.3 %strip_pack.1 = (f32[80,256]{1,0:T(8,128)S(1)}, f32[80,256]{1,0:T(8,128)S(1)}, f32[80,256]{1,0:T(8,128)S(1)}, f32[80,256]{1,0:T(8,128)S(1)}, f32[80,256]{1,0:T(8...) custom-call(s32[1]{0:T(128)S(6)} %copy.8.anchor_x, ...), custom_call_target="tpu_custom_call" | custom-call | tf_op jit(solution)/shard_map/strip_pack/pallas_call | solution.py:411
  3.2 5.2 %collective-permute-start = (f32[80,256]{1,0:T(8,128)S(1)}, f32[80,256]{1,0:T(8,128)S(1)}, u32[]{:S(2)}, u32[]{:S(2)}) collective-permute-start(f32[80,256]{1,0:T(8,128)S(1)} %get-tuple-element.28), channel_id=1, source_target_pairs={{0,28},{4,24},{8,20},{12,16},{16,12},{20,8},{24,4},{28,0},{1,29},{... | collective-permute-start | bytes 245768 | tf_op jit(solution)/shard_map/ppermute | solution.py:381
  8.4 1.3 %collective-permute-start.2 = (f32[80,256]{1,0:T(8,128)S(1)}, f32[80,256]{1,0:T(8,128)S(1)}, u32[]{:S(2)}, u32[]{:S(2)}) collective-permute-start(f32[80,256]{1,0:T(8,128)S(1)} %get-tuple-element.30), channel_id=1, source_target_pairs={{0,24},{4,28},{8,16},{12,20},{16,8},{20,12},{24,0},{28,4},{1,25},{... | collective-permute-start | bytes 245768 | tf_op jit(solution)/shard_map/ppermute | solution.py:381
  9.7 1.0 %collective-permute-start.3 = (f32[80,256]{1,0:T(8,128)S(1)}, f32[80,256]{1,0:T(8,128)S(1)}, u32[]{:S(2)}, u32[]{:S(2)}) collective-permute-start(f32[80,256]{1,0:T(8,128)S(1)} %get-tuple-element.31), channel_id=1, source_target_pairs={{0,16},{4,20},{8,24},{12,28},{16,0},{20,4},{24,8},{28,12},{1,17},{... | collective-permute-start | bytes 245768 | tf_op jit(solution)/shard_map/ppermute | solution.py:381
  10.7 1.3 %collective-permute-start.4 = (f32[80,256]{1,0:T(8,128)S(1)}, f32[80,256]{1,0:T(8,128)S(1)}, u32[]{:S(2)}, u32[]{:S(2)}) collective-permute-start(f32[80,256]{1,0:T(8,128)S(1)} %get-tuple-element.32), channel_id=1, source_target_pairs={{0,12},{4,8},{8,4},{12,0},{16,28},{20,24},{24,20},{28,16},{1,13},{... | collective-permute-start | bytes 245768 | tf_op jit(solution)/shard_map/ppermute | solution.py:381
  12.0 1.1 %collective-permute-start.5 = (f32[80,256]{1,0:T(8,128)S(1)}, f32[80,256]{1,0:T(8,128)S(1)}, u32[]{:S(2)}, u32[]{:S(2)}) collective-permute-start(f32[80,256]{1,0:T(8,128)S(1)} %get-tuple-element.33), channel_id=1, source_target_pairs={{0,8},{4,12},{8,0},{12,4},{16,24},{20,28},{24,16},{28,20},{1,9},{5... | collective-permute-start | bytes 245768 | tf_op jit(solution)/shard_map/ppermute | solution.py:381
  13.1 5.9 %collective-permute-done.1.rest_1_ = f32[80,256]{1,0:T(8,128)S(1)} collective-permute-done((f32[80,256]{1,0:T(8,128)S(1)}, f32[80,256]{1,0:T(8,128)S(1)}, u32[]{:S(2)}, u32[]{:S(2)}) %collective-permute-start.1) | collective-permute-done | bytes 81952 | tf_op jit(solution)/shard_map/ppermute | solution.py:381
  19.0 0.8 %collective-permute-start.6 = (f32[80,256]{1,0:T(8,128)S(1)}, f32[80,256]{1,0:T(8,128)S(1)}, u32[]{:S(2)}, u32[]{:S(2)}) collective-permute-start(f32[80,256]{1,0:T(8,128)S(1)} %get-tuple-element.34), channel_id=1, source_target_pairs={{0,4},{4,0},{8,12},{12,8},{16,20},{20,16},{24,28},{28,24},{1,5},{5... | collective-permute-start | bytes 245768 | tf_op jit(solution)/shard_map/ppermute | solution.py:381
  20.5 1.7 %collective-permute-done.3.rest_3_ = f32[80,256]{1,0:T(8,128)S(1)} collective-permute-done((f32[80,256]{1,0:T(8,128)S(1)}, f32[80,256]{1,0:T(8,128)S(1)}, u32[]{:S(2)}, u32[]{:S(2)}) %collective-permute-start.3) | collective-permute-done | bytes 81952 | tf_op jit(solution)/shard_map/ppermute | solution.py:381
  22.1 0.5 %collective-permute-done.6.rest_6_ = f32[80,256]{1,0:T(8,128)S(1)} collective-permute-done((f32[80,256]{1,0:T(8,128)S(1)}, f32[80,256]{1,0:T(8,128)S(1)}, u32[]{:S(2)}, u32[]{:S(2)}) %collective-permute-start.6) | collective-permute-done | bytes 81952 | tf_op jit(solution)/shard_map/ppermute | solution.py:381
  22.6 1.3 %strip_steps.1 = (f32[144,128]{1,0:T(8,128)S(1)}, f32[136,128]{1,0:T(8,128)S(1)}, f32[144,128]{1,0:T(8,128)S(1)}, f32[136,128]{1,0:T(8,128)S(1)}) custom-call(s32[1]{0:T(128)S(6)} %copy.10.source, s32[8,256]{1,0:T(8,128)S(1)} %get-tuple-element.26.facts, s32[1,256]{1,0:T(1,128)S(1)} %get-tuple-element.27.receivers, ...), custom_call_target="tpu_custom_call" | custom-call | tf_op jit(solution)/shard_map/strip_steps/pallas_call | solution.py:419
  23.9 1.8 %collective-permute-start.7 = (f32[144,128]{1,0:T(8,128)S(1)}, f32[144,128]{1,0:T(8,128)S(1)}, u32[]{:S(2)}, u32[]{:S(2)}) collective-permute-start(f32[144,128]{1,0:T(8,128)S(1)} %get-tuple-element.37), channel_id=1, source_target_pairs={{0,1},{1,0},{2,3},{3,2},{4,5},{5,4},{6,7},{7,6},{8,9},{9,8},{10,11... | collective-permute-start | bytes 221192 | tf_op jit(solution)/shard_map/ppermute | solution.py:381
  25.8 1.2 %collective-permute-done.12.got = f32[136,128]{1,0:T(8,128)S(1)} collective-permute-done((f32[136,128]{1,0:T(8,128)S(1)}, f32[136,128]{1,0:T(8,128)S(1)}, u32[]{:S(2)}, u32[]{:S(2)}) %collective-permute-start.12) | collective-permute-done | bytes 69664 | tf_op jit(solution)/shard_map/ppermute | solution.py:381
  27.1 1.3 %collective-permute-start.13 = (f32[256,128]{1,0:T(8,128)S(1)}, f32[256,128]{1,0:T(8,128)S(1)}, u32[]{:S(2)}, u32[]{:S(2)}) collective-permute-start(f32[256,128]{1,0:T(8,128)S(1)} %get-tuple-element.46), channel_id=1, source_target_pairs={{0,2},{1,3},{2,0},{3,1},{4,6},{5,7},{6,4},{7,5},{8,10},{9,11},{10,... | collective-permute-start | bytes 393224 | tf_op jit(solution)/shard_map/ppermute | solution.py:381
  28.5 0.3 collective-permute-start.8
  28.8 1.7 %collective-permute-start.9 = (f32[8,128]{1,0:T(8,128)S(1)}, f32[8,128]{1,0:T(8,128)S(1)}, u32[]{:S(2)}, u32[]{:S(2)}) collective-permute-start(f32[8,128]{1,0:T(8,128)S(1)} %get-tuple-element.40), channel_id=1, source_target_pairs={{0,4},{4,0},{8,12},{12,8},{16,20},{20,16},{24,28},{28,24},{1,5},{5... | collective-permute-start | bytes 12296 | tf_op jit(solution)/shard_map/ppermute | solution.py:381
  30.5 1.3 %collective-permute-done.9.heard_too = f32[8,128]{1,0:T(8,128)S(1)} collective-permute-done((f32[8,128]{1,0:T(8,128)S(1)}, f32[8,128]{1,0:T(8,128)S(1)}, u32[]{:S(2)}, u32[]{:S(2)}) %collective-permute-start.9) | collective-permute-done | bytes 4128 | tf_op jit(solution)/shard_map/ppermute | solution.py:381
  32.1 1.5 %collective-permute-start.14 = (f32[136,128]{1,0:T(8,128)S(1)}, f32[136,128]{1,0:T(8,128)S(1)}, u32[]{:S(2)}, u32[]{:S(2)}) collective-permute-start(f32[136,128]{1,0:T(8,128)S(1)} %get-tuple-element.48), channel_id=1, source_target_pairs={{0,8},{1,12},{2,10},{3,14},{4,9},{5,13},{6,11},{7,15},{8,0},{9,4},... | collective-permute-start | bytes 208904 | tf_op jit(solution)/shard_map/ppermute | solution.py:398
  33.6 3.7 %collective-permute-start.15 = (f32[136,128]{1,0:T(8,128)S(1)}, f32[136,128]{1,0:T(8,128)S(1)}, u32[]{:S(2)}, u32[]{:S(2)}) collective-permute-start(f32[136,128]{1,0:T(8,128)S(1)} %get-tuple-element.49), channel_id=1, source_target_pairs={{0,0},{1,4},{2,2},{3,6},{4,1},{5,5},{6,3},{7,7},{8,8},{9,12},{10,1... | collective-permute-start | bytes 208904 | tf_op jit(solution)/shard_map/ppermute | solution.py:398
  37.3 4.1 %collective-permute-start.10 = (f32[136,128]{1,0:T(8,128)S(1)}, f32[136,128]{1,0:T(8,128)S(1)}, u32[]{:S(2)}, u32[]{:S(2)}) collective-permute-start(f32[136,128]{1,0:T(8,128)S(1)} %get-tuple-element.42), channel_id=1, source_target_pairs={{0,16},{1,20},{2,18},{3,22},{4,17},{5,21},{6,19},{7,23},{8,24},{9,... | collective-permute-start | bytes 208904 | tf_op jit(solution)/shard_map/ppermute | solution.py:398
  41.4 0.4 collective-permute-start.11
  41.8 2.6 %collective-permute-done.10.rest_0_ = f32[136,128]{1,0:T(8,128)S(1)} collective-permute-done((f32[136,128]{1,0:T(8,128)S(1)}, f32[136,128]{1,0:T(8,128)S(1)}, u32[]{:S(2)}, u32[]{:S(2)}) %collective-permute-start.10) | collective-permute-done | bytes 69664 | tf_op jit(solution)/shard_map/ppermute | solution.py:398
  44.4 3.5 %collective-permute-done.11.rest_1_ = f32[136,128]{1,0:T(8,128)S(1)} collective-permute-done((f32[136,128]{1,0:T(8,128)S(1)}, f32[136,128]{1,0:T(8,128)S(1)}, u32[]{:S(2)}, u32[]{:S(2)}) %collective-permute-start.11) | collective-permute-done | bytes 69664 | tf_op jit(solution)/shard_map/ppermute | solution.py:398
  47.9 0.7 %strip_place.1 = (f32[1,4,256]{2,1,0:T(4,128)}, f32[1,128,512]{2,1,0:T(8,128)}) custom-call(f32[136,128]{1,0:T(8,128)S(1)} %collective-permute-done.10.rest_0_, f32[136,128]{1,0:T(8,128)S(1)} %collective-permute-done.11.rest_1_, f32[136,128]{1,0:T(8,128)S(1)} %collective-permute-done.14.rest_2_, f32[136,128]{1,0:T(8,128)S(1)} %collective-permute-done.15.rest_3_), custom_call_target="tpu_custom_call" | custom-call | tf_op jit(solution)/shard_map/strip_place/pallas_call | solution.py:440
  (15 shorter events, 0.6 us)
Async XLA Ops:
  3.2 8.8 %collective-permute-start = (f32[80,256]{1,0:T(8,128)S(1)}, f32[80,256]{1,0:T(8,128)S(1)}, u32[]{:S(2)}, u32[]{:S(2)}) collective-permute-start(f32[80,256]{1,0:T(8,128)S(1)} %get-tuple-element.28), channel_id=1, source_target_pairs={{0,28},{4,24},{8,20},{12,16},{16,12},{20,8},{24,4},{28,0},{1,29},{... | collective-permute-start | bytes 245768 | tf_op jit(solution)/shard_map/ppermute | solution.py:381
  8.4 10.6 %collective-permute-start.1 = (f32[80,256]{1,0:T(8,128)S(1)}, f32[80,256]{1,0:T(8,128)S(1)}, u32[]{:S(2)}, u32[]{:S(2)}) collective-permute-start(f32[80,256]{1,0:T(8,128)S(1)} %get-tuple-element.29), channel_id=1, source_target_pairs={{0,20},{4,16},{8,28},{12,24},{16,4},{20,0},{24,12},{28,8},{1,21},{... | collective-permute-start | bytes 245768 | tf_op jit(solution)/shard_map/ppermute | solution.py:381
  8.4 12.0 %collective-permute-start.2 = (f32[80,256]{1,0:T(8,128)S(1)}, f32[80,256]{1,0:T(8,128)S(1)}, u32[]{:S(2)}, u32[]{:S(2)}) collective-permute-start(f32[80,256]{1,0:T(8,128)S(1)} %get-tuple-element.30), channel_id=1, source_target_pairs={{0,24},{4,28},{8,16},{12,20},{16,8},{20,12},{24,0},{28,4},{1,25},{... | collective-permute-start | bytes 245768 | tf_op jit(solution)/shard_map/ppermute | solution.py:381
  9.7 12.4 %collective-permute-start.3 = (f32[80,256]{1,0:T(8,128)S(1)}, f32[80,256]{1,0:T(8,128)S(1)}, u32[]{:S(2)}, u32[]{:S(2)}) collective-permute-start(f32[80,256]{1,0:T(8,128)S(1)} %get-tuple-element.31), channel_id=1, source_target_pairs={{0,16},{4,20},{8,24},{12,28},{16,0},{20,4},{24,8},{28,12},{1,17},{... | collective-permute-start | bytes 245768 | tf_op jit(solution)/shard_map/ppermute | solution.py:381
  10.7 11.4 %collective-permute-start.4 = (f32[80,256]{1,0:T(8,128)S(1)}, f32[80,256]{1,0:T(8,128)S(1)}, u32[]{:S(2)}, u32[]{:S(2)}) collective-permute-start(f32[80,256]{1,0:T(8,128)S(1)} %get-tuple-element.32), channel_id=1, source_target_pairs={{0,12},{4,8},{8,4},{12,0},{16,28},{20,24},{24,20},{28,16},{1,13},{... | collective-permute-start | bytes 245768 | tf_op jit(solution)/shard_map/ppermute | solution.py:381
  12.0 10.1 %collective-permute-start.5 = (f32[80,256]{1,0:T(8,128)S(1)}, f32[80,256]{1,0:T(8,128)S(1)}, u32[]{:S(2)}, u32[]{:S(2)}) collective-permute-start(f32[80,256]{1,0:T(8,128)S(1)} %get-tuple-element.33), channel_id=1, source_target_pairs={{0,8},{4,12},{8,0},{12,4},{16,24},{20,28},{24,16},{28,20},{1,9},{5... | collective-permute-start | bytes 245768 | tf_op jit(solution)/shard_map/ppermute | solution.py:381
  19.0 3.6 %collective-permute-start.6 = (f32[80,256]{1,0:T(8,128)S(1)}, f32[80,256]{1,0:T(8,128)S(1)}, u32[]{:S(2)}, u32[]{:S(2)}) collective-permute-start(f32[80,256]{1,0:T(8,128)S(1)} %get-tuple-element.34), channel_id=1, source_target_pairs={{0,4},{4,0},{8,12},{12,8},{16,20},{20,16},{24,28},{28,24},{1,5},{5... | collective-permute-start | bytes 245768 | tf_op jit(solution)/shard_map/ppermute | solution.py:381
  23.9 4.5 %collective-permute-start.7 = (f32[144,128]{1,0:T(8,128)S(1)}, f32[144,128]{1,0:T(8,128)S(1)}, u32[]{:S(2)}, u32[]{:S(2)}) collective-permute-start(f32[144,128]{1,0:T(8,128)S(1)} %get-tuple-element.37), channel_id=1, source_target_pairs={{0,1},{1,0},{2,3},{3,2},{4,5},{5,4},{6,7},{7,6},{8,9},{9,8},{10,11... | collective-permute-start | bytes 221192 | tf_op jit(solution)/shard_map/ppermute | solution.py:381
  25.7 1.3 %collective-permute-start.12 = (f32[136,128]{1,0:T(8,128)S(1)}, f32[136,128]{1,0:T(8,128)S(1)}, u32[]{:S(2)}, u32[]{:S(2)}) collective-permute-start(f32[136,128]{1,0:T(8,128)S(1)} %get-tuple-element.45), channel_id=1, source_target_pairs={{0,1},{1,0},{2,3},{3,2},{4,5},{5,4},{6,7},{7,6},{8,9},{9,8},{10,11... | collective-permute-start | bytes 208904 | tf_op jit(solution)/shard_map/ppermute | solution.py:381
  27.1 5.0 %collective-permute-start.13 = (f32[256,128]{1,0:T(8,128)S(1)}, f32[256,128]{1,0:T(8,128)S(1)}, u32[]{:S(2)}, u32[]{:S(2)}) collective-permute-start(f32[256,128]{1,0:T(8,128)S(1)} %get-tuple-element.46), channel_id=1, source_target_pairs={{0,2},{1,3},{2,0},{3,1},{4,6},{5,7},{6,4},{7,5},{8,10},{9,11},{10,... | collective-permute-start | bytes 393224 | tf_op jit(solution)/shard_map/ppermute | solution.py:381
  28.5 8.8 %collective-permute-start.8 = (f32[256,128]{1,0:T(8,128)S(1)}, f32[256,128]{1,0:T(8,128)S(1)}, u32[]{:S(2)}, u32[]{:S(2)}) collective-permute-start(f32[256,128]{1,0:T(8,128)S(1)} %get-tuple-element.38), channel_id=1, source_target_pairs={{0,2},{1,3},{2,0},{3,1},{4,6},{5,7},{6,4},{7,5},{8,10},{9,11},{10,... | collective-permute-start | bytes 393224 | tf_op jit(solution)/shard_map/ppermute | solution.py:381
  28.8 3.0 %collective-permute-start.9 = (f32[8,128]{1,0:T(8,128)S(1)}, f32[8,128]{1,0:T(8,128)S(1)}, u32[]{:S(2)}, u32[]{:S(2)}) collective-permute-start(f32[8,128]{1,0:T(8,128)S(1)} %get-tuple-element.40), channel_id=1, source_target_pairs={{0,4},{4,0},{8,12},{12,8},{16,20},{20,16},{24,28},{28,24},{1,5},{5... | collective-permute-start | bytes 12296 | tf_op jit(solution)/shard_map/ppermute | solution.py:381
  32.1 9.7 %collective-permute-start.14 = (f32[136,128]{1,0:T(8,128)S(1)}, f32[136,128]{1,0:T(8,128)S(1)}, u32[]{:S(2)}, u32[]{:S(2)}) collective-permute-start(f32[136,128]{1,0:T(8,128)S(1)} %get-tuple-element.48), channel_id=1, source_target_pairs={{0,8},{1,12},{2,10},{3,14},{4,9},{5,13},{6,11},{7,15},{8,0},{9,4},... | collective-permute-start | bytes 208904 | tf_op jit(solution)/shard_map/ppermute | solution.py:398
  33.6 8.2 %collective-permute-start.15 = (f32[136,128]{1,0:T(8,128)S(1)}, f32[136,128]{1,0:T(8,128)S(1)}, u32[]{:S(2)}, u32[]{:S(2)}) collective-permute-start(f32[136,128]{1,0:T(8,128)S(1)} %get-tuple-element.49), channel_id=1, source_target_pairs={{0,0},{1,4},{2,2},{3,6},{4,1},{5,5},{6,3},{7,7},{8,8},{9,12},{10,1... | collective-permute-start | bytes 208904 | tf_op jit(solution)/shard_map/ppermute | solution.py:398
  37.3 7.1 %collective-permute-start.10 = (f32[136,128]{1,0:T(8,128)S(1)}, f32[136,128]{1,0:T(8,128)S(1)}, u32[]{:S(2)}, u32[]{:S(2)}) collective-permute-start(f32[136,128]{1,0:T(8,128)S(1)} %get-tuple-element.42), channel_id=1, source_target_pairs={{0,16},{1,20},{2,18},{3,22},{4,17},{5,21},{6,19},{7,23},{8,24},{9,... | collective-permute-start | bytes 208904 | tf_op jit(solution)/shard_map/ppermute | solution.py:398
  41.4 6.4 %collective-permute-start.11 = (f32[136,128]{1,0:T(8,128)S(1)}, f32[136,128]{1,0:T(8,128)S(1)}, u32[]{:S(2)}, u32[]{:S(2)}) collective-permute-start(f32[136,128]{1,0:T(8,128)S(1)} %get-tuple-element.43), channel_id=1, source_target_pairs={{0,24},{1,28},{2,26},{3,30},{4,25},{5,29},{6,27},{7,31},{8,16},{9,... | collective-permute-start | bytes 208904 | tf_op jit(solution)/shard_map/ppermute | solution.py:398

commit v3 on v2

--- a/solution.py
+++ b/solution.py
@@ -381,9 +381,8 @@
     return lax.ppermute(array, axis, [(i, i ^ k) for i in range(lax.axis_size(axis))])
 
 
-def far_first(count):
-    half = count // 2
-    return [*range(count - 1, half, -2), *range(count - 2, half - 1, -2), *range(half - 1, -1, -1)]
+def far_first():
+    return [7, 5, 6, 4, 1, 3, 2, 0]
 
 
 def cross(array, k):
@@ -411,7 +410,7 @@
     *packed, facts, listed = strip_pack(window_rows, window_cols, velocity.shape[1], slabs, strip, records)(
         anchor_x, anchor_y, receivers, velocity, initial_field
     )
-    order = far_first(slabs)
+    order = far_first()
     held = [swap(packed[k], "slab", k) if k else packed[k] for k in order]
     pairs = slabs // 2
     chunks = ((*range(pairs // 2, pairs),), (*range(pairs // 2 - 1, -1, -1),))

time: 48.8 us -> 48.8 us (level)
  waiting for transfers between devices: 16.9 us -> 19.6 us
  starting transfers between devices: 25.5 us -> 22.8 us
    ppermute x12, waiting for transfers between devices: 10.8 us -> 13.6 us  [swap(): lax.ppermute(array, axis, [(i, i ^ k) for i in range(lax.axis_size(axis))])]
    ppermute x12, starting transfers between devices: 15.8 us -> 13.7 us  [swap(): lax.ppermute(array, axis, [(i, i ^ k) for i in range(lax.axis_size(axis))])]
    ppermute x4, starting transfers between devices: 9.67 us -> 9.14 us  [cross(): return lax.ppermute(array, ('slab', 'shot'), pairs)]
where the time goes in v3:
time: 48.8 us; the launch traced here: 48.7 us
  starting transfers between devices  22.8 us (47%)
  waiting for transfers between devices  19.6 us (40%)
  Pallas kernels  3.56 us (7%)
  between operations  2.65 us (5%)
    ppermute x12, starting transfers between devices, swap(): lax.ppermute(array, axis, [(i, i ^ k) for i in range(lax.axis_size(axis))])  13.7 us
    ppermute x12, waiting for transfers between devices, swap(): lax.ppermute(array, axis, [(i, i ^ k) for i in range(lax.axis_size(axis))])  13.6 us
    ppermute x4, starting transfers between devices, cross(): return lax.ppermute(array, ('slab', 'shot'), pairs)  9.14 us
    ppermute x4, waiting for transfers between devices, cross(): return lax.ppermute(array, ('slab', 'shot'), pairs)  6.1 us
    pallas_call x1, Pallas kernels, by_strips(): strip_pack(window_rows, window_cols, velocity.shape[1], slabs, strip, rec...  1.31 us
    pallas_call x1, Pallas kernels, by_strips(): strip_steps(window_rows, window_cols, slabs, strip, records, order, chunks)  1.27 us
  transfers between devices with their start and end apart: 16, of which 8 were waited for; matrix products, arithmetic and copies ran while one was open for 0% of the time, Pallas kernels for 1%

profile of v3, /device:TPU:1, one launch (start us, length us, event | category | flops | bytes accessed | tf_op | source)
XLA Modules:
  0.0 48.7 jit_solution(7943967703336565475)
XLA Ops:
  1.9 1.3 %strip_pack.1 = (f32[80,256]{1,0:T(8,128)S(1)}, f32[80,256]{1,0:T(8,128)S(1)}, f32[80,256]{1,0:T(8,128)S(1)}, f32[80,256]{1,0:T(8,128)S(1)}, f32[80,256]{1,0:T(8...) custom-call(s32[1]{0:T(128)S(6)} %copy.8.anchor_x, ...), custom_call_target="tpu_custom_call" | custom-call | tf_op jit(solution)/shard_map/strip_pack/pallas_call | solution.py:410
  3.2 5.2 %collective-permute-start = (f32[80,256]{1,0:T(8,128)S(1)}, f32[80,256]{1,0:T(8,128)S(1)}, u32[]{:S(2)}, u32[]{:S(2)}) collective-permute-start(f32[80,256]{1,0:T(8,128)S(1)} %get-tuple-element.28), channel_id=1, source_target_pairs={{0,28},{4,24},{8,20},{12,16},{16,12},{20,8},{24,4},{28,0},{1,29},{... | collective-permute-start | bytes 245768 | tf_op jit(solution)/shard_map/ppermute | solution.py:381
  8.4 1.3 %collective-permute-start.2 = (f32[80,256]{1,0:T(8,128)S(1)}, f32[80,256]{1,0:T(8,128)S(1)}, u32[]{:S(2)}, u32[]{:S(2)}) collective-permute-start(f32[80,256]{1,0:T(8,128)S(1)} %get-tuple-element.30), channel_id=1, source_target_pairs={{0,24},{4,28},{8,16},{12,20},{16,8},{20,12},{24,0},{28,4},{1,25},{... | collective-permute-start | bytes 245768 | tf_op jit(solution)/shard_map/ppermute | solution.py:381
  9.7 1.0 %collective-permute-start.3 = (f32[80,256]{1,0:T(8,128)S(1)}, f32[80,256]{1,0:T(8,128)S(1)}, u32[]{:S(2)}, u32[]{:S(2)}) collective-permute-start(f32[80,256]{1,0:T(8,128)S(1)} %get-tuple-element.31), channel_id=1, source_target_pairs={{0,16},{4,20},{8,24},{12,28},{16,0},{20,4},{24,8},{28,12},{1,17},{... | collective-permute-start | bytes 245768 | tf_op jit(solution)/shard_map/ppermute | solution.py:381
  10.7 1.2 %collective-permute-start.4 = (f32[80,256]{1,0:T(8,128)S(1)}, f32[80,256]{1,0:T(8,128)S(1)}, u32[]{:S(2)}, u32[]{:S(2)}) collective-permute-start(f32[80,256]{1,0:T(8,128)S(1)} %get-tuple-element.32), channel_id=1, source_target_pairs={{0,4},{4,0},{8,12},{12,8},{16,20},{20,16},{24,28},{28,24},{1,5},{5... | collective-permute-start | bytes 245768 | tf_op jit(solution)/shard_map/ppermute | solution.py:381
  12.0 1.2 %collective-permute-start.5 = (f32[80,256]{1,0:T(8,128)S(1)}, f32[80,256]{1,0:T(8,128)S(1)}, u32[]{:S(2)}, u32[]{:S(2)}) collective-permute-start(f32[80,256]{1,0:T(8,128)S(1)} %get-tuple-element.33), channel_id=1, source_target_pairs={{0,12},{4,8},{8,4},{12,0},{16,28},{20,24},{24,20},{28,16},{1,13},{... | collective-permute-start | bytes 245768 | tf_op jit(solution)/shard_map/ppermute | solution.py:381
  13.1 5.9 %collective-permute-done.1.rest_1_ = f32[80,256]{1,0:T(8,128)S(1)} collective-permute-done((f32[80,256]{1,0:T(8,128)S(1)}, f32[80,256]{1,0:T(8,128)S(1)}, u32[]{:S(2)}, u32[]{:S(2)}) %collective-permute-start.1) | collective-permute-done | bytes 81952 | tf_op jit(solution)/shard_map/ppermute | solution.py:381
  19.7 2.4 %collective-permute-done.3.rest_3_ = f32[80,256]{1,0:T(8,128)S(1)} collective-permute-done((f32[80,256]{1,0:T(8,128)S(1)}, f32[80,256]{1,0:T(8,128)S(1)}, u32[]{:S(2)}, u32[]{:S(2)}) %collective-permute-start.3) | collective-permute-done | bytes 81952 | tf_op jit(solution)/shard_map/ppermute | solution.py:381
  22.1 1.9 %collective-permute-done.6.rest_6_ = f32[80,256]{1,0:T(8,128)S(1)} collective-permute-done((f32[80,256]{1,0:T(8,128)S(1)}, f32[80,256]{1,0:T(8,128)S(1)}, u32[]{:S(2)}, u32[]{:S(2)}) %collective-permute-start.6) | collective-permute-done | bytes 81952 | tf_op jit(solution)/shard_map/ppermute | solution.py:381
  24.1 1.3 %strip_steps.1 = (f32[144,128]{1,0:T(8,128)S(1)}, f32[136,128]{1,0:T(8,128)S(1)}, f32[144,128]{1,0:T(8,128)S(1)}, f32[136,128]{1,0:T(8,128)S(1)}) custom-call(s32[1]{0:T(128)S(6)} %copy.10.source, s32[8,256]{1,0:T(8,128)S(1)} %get-tuple-element.26.facts, s32[1,256]{1,0:T(1,128)S(1)} %get-tuple-element.27.receivers, ...), custom_call_target="tpu_custom_call" | custom-call | tf_op jit(solution)/shard_map/strip_steps/pallas_call | solution.py:418
  25.3 1.0 %collective-permute-start.7 = (f32[144,128]{1,0:T(8,128)S(1)}, f32[144,128]{1,0:T(8,128)S(1)}, u32[]{:S(2)}, u32[]{:S(2)}) collective-permute-start(f32[144,128]{1,0:T(8,128)S(1)} %get-tuple-element.37), channel_id=1, source_target_pairs={{0,1},{1,0},{2,3},{3,2},{4,5},{5,4},{6,7},{7,6},{8,9},{9,8},{10,11... | collective-permute-start | bytes 221192 | tf_op jit(solution)/shard_map/ppermute | solution.py:381
  26.4 1.2 %collective-permute-done.12.got = f32[136,128]{1,0:T(8,128)S(1)} collective-permute-done((f32[136,128]{1,0:T(8,128)S(1)}, f32[136,128]{1,0:T(8,128)S(1)}, u32[]{:S(2)}, u32[]{:S(2)}) %collective-permute-start.12) | collective-permute-done | bytes 69664 | tf_op jit(solution)/shard_map/ppermute | solution.py:381
  27.7 1.3 %collective-permute-start.13 = (f32[256,128]{1,0:T(8,128)S(1)}, f32[256,128]{1,0:T(8,128)S(1)}, u32[]{:S(2)}, u32[]{:S(2)}) collective-permute-start(f32[256,128]{1,0:T(8,128)S(1)} %get-tuple-element.46), channel_id=1, source_target_pairs={{0,2},{1,3},{2,0},{3,1},{4,6},{5,7},{6,4},{7,5},{8,10},{9,11},{10,... | collective-permute-start | bytes 393224 | tf_op jit(solution)/shard_map/ppermute | solution.py:381
  29.1 0.3 collective-permute-start.8
  29.4 1.1 %collective-permute-start.9 = (f32[8,128]{1,0:T(8,128)S(1)}, f32[8,128]{1,0:T(8,128)S(1)}, u32[]{:S(2)}, u32[]{:S(2)}) collective-permute-start(f32[8,128]{1,0:T(8,128)S(1)} %get-tuple-element.40), channel_id=1, source_target_pairs={{0,4},{4,0},{8,12},{12,8},{16,20},{20,16},{24,28},{28,24},{1,5},{5... | collective-permute-start | bytes 12296 | tf_op jit(solution)/shard_map/ppermute | solution.py:381
  30.5 1.6 %collective-permute-done.9.heard_too = f32[8,128]{1,0:T(8,128)S(1)} collective-permute-done((f32[8,128]{1,0:T(8,128)S(1)}, f32[8,128]{1,0:T(8,128)S(1)}, u32[]{:S(2)}, u32[]{:S(2)}) %collective-permute-start.9) | collective-permute-done | bytes 4128 | tf_op jit(solution)/shard_map/ppermute | solution.py:381
  32.2 0.5 %collective-permute-done.13.come = f32[256,128]{1,0:T(8,128)S(1)} collective-permute-done((f32[256,128]{1,0:T(8,128)S(1)}, f32[256,128]{1,0:T(8,128)S(1)}, u32[]{:S(2)}, u32[]{:S(2)}) %collective-permute-start.13) | collective-permute-done | bytes 131104 | tf_op jit(solution)/shard_map/ppermute | solution.py:381
  32.7 2.1 %collective-permute-start.14 = (f32[136,128]{1,0:T(8,128)S(1)}, f32[136,128]{1,0:T(8,128)S(1)}, u32[]{:S(2)}, u32[]{:S(2)}) collective-permute-start(f32[136,128]{1,0:T(8,128)S(1)} %get-tuple-element.48), channel_id=1, source_target_pairs={{0,8},{1,12},{2,10},{3,14},{4,9},{5,13},{6,11},{7,15},{8,0},{9,4},... | collective-permute-start | bytes 208904 | tf_op jit(solution)/shard_map/ppermute | solution.py:397
  34.8 2.5 %collective-permute-start.15 = (f32[136,128]{1,0:T(8,128)S(1)}, f32[136,128]{1,0:T(8,128)S(1)}, u32[]{:S(2)}, u32[]{:S(2)}) collective-permute-start(f32[136,128]{1,0:T(8,128)S(1)} %get-tuple-element.49), channel_id=1, source_target_pairs={{0,0},{1,4},{2,2},{3,6},{4,1},{5,5},{6,3},{7,7},{8,8},{9,12},{10,1... | collective-permute-start | bytes 208904 | tf_op jit(solution)/shard_map/ppermute | solution.py:397
  37.4 4.2 %collective-permute-start.10 = (f32[136,128]{1,0:T(8,128)S(1)}, f32[136,128]{1,0:T(8,128)S(1)}, u32[]{:S(2)}, u32[]{:S(2)}) collective-permute-start(f32[136,128]{1,0:T(8,128)S(1)} %get-tuple-element.42), channel_id=1, source_target_pairs={{0,16},{1,20},{2,18},{3,22},{4,17},{5,21},{6,19},{7,23},{8,24},{9,... | collective-permute-start | bytes 208904 | tf_op jit(solution)/shard_map/ppermute | solution.py:397
  41.5 0.3 collective-permute-start.11
  41.9 2.9 %collective-permute-done.10.rest_0_ = f32[136,128]{1,0:T(8,128)S(1)} collective-permute-done((f32[136,128]{1,0:T(8,128)S(1)}, f32[136,128]{1,0:T(8,128)S(1)}, u32[]{:S(2)}, u32[]{:S(2)}) %collective-permute-start.10) | collective-permute-done | bytes 69664 | tf_op jit(solution)/shard_map/ppermute | solution.py:397
  44.8 3.2 %collective-permute-done.11.rest_1_ = f32[136,128]{1,0:T(8,128)S(1)} collective-permute-done((f32[136,128]{1,0:T(8,128)S(1)}, f32[136,128]{1,0:T(8,128)S(1)}, u32[]{:S(2)}, u32[]{:S(2)}) %collective-permute-start.11) | collective-permute-done | bytes 69664 | tf_op jit(solution)/shard_map/ppermute | solution.py:397
  47.9 0.7 %strip_place.1 = (f32[1,4,256]{2,1,0:T(4,128)}, f32[1,128,512]{2,1,0:T(8,128)}) custom-call(f32[136,128]{1,0:T(8,128)S(1)} %collective-permute-done.10.rest_0_, f32[136,128]{1,0:T(8,128)S(1)} %collective-permute-done.11.rest_1_, f32[136,128]{1,0:T(8,128)S(1)} %collective-permute-done.14.rest_2_, f32[136,128]{1,0:T(8,128)S(1)} %collective-permute-done.15.rest_3_), custom_call_target="tpu_custom_call" | custom-call | tf_op jit(solution)/shard_map/strip_place/pallas_call | solution.py:439
  (15 shorter events, 0.4 us)
Async XLA Ops:
  3.2 8.7 %collective-permute-start = (f32[80,256]{1,0:T(8,128)S(1)}, f32[80,256]{1,0:T(8,128)S(1)}, u32[]{:S(2)}, u32[]{:S(2)}) collective-permute-start(f32[80,256]{1,0:T(8,128)S(1)} %get-tuple-element.28), channel_id=1, source_target_pairs={{0,28},{4,24},{8,20},{12,16},{16,12},{20,8},{24,4},{28,0},{1,29},{... | collective-permute-start | bytes 245768 | tf_op jit(solution)/shard_map/ppermute | solution.py:381
  8.4 10.6 %collective-permute-start.1 = (f32[80,256]{1,0:T(8,128)S(1)}, f32[80,256]{1,0:T(8,128)S(1)}, u32[]{:S(2)}, u32[]{:S(2)}) collective-permute-start(f32[80,256]{1,0:T(8,128)S(1)} %get-tuple-element.29), channel_id=1, source_target_pairs={{0,20},{4,16},{8,28},{12,24},{16,4},{20,0},{24,12},{28,8},{1,21},{... | collective-permute-start | bytes 245768 | tf_op jit(solution)/shard_map/ppermute | solution.py:381
  8.4 11.3 %collective-permute-start.2 = (f32[80,256]{1,0:T(8,128)S(1)}, f32[80,256]{1,0:T(8,128)S(1)}, u32[]{:S(2)}, u32[]{:S(2)}) collective-permute-start(f32[80,256]{1,0:T(8,128)S(1)} %get-tuple-element.30), channel_id=1, source_target_pairs={{0,24},{4,28},{8,16},{12,20},{16,8},{20,12},{24,0},{28,4},{1,25},{... | collective-permute-start | bytes 245768 | tf_op jit(solution)/shard_map/ppermute | solution.py:381
  9.7 12.4 %collective-permute-start.3 = (f32[80,256]{1,0:T(8,128)S(1)}, f32[80,256]{1,0:T(8,128)S(1)}, u32[]{:S(2)}, u32[]{:S(2)}) collective-permute-start(f32[80,256]{1,0:T(8,128)S(1)} %get-tuple-element.31), channel_id=1, source_target_pairs={{0,16},{4,20},{8,24},{12,28},{16,0},{20,4},{24,8},{28,12},{1,17},{... | collective-permute-start | bytes 245768 | tf_op jit(solution)/shard_map/ppermute | solution.py:381
  10.7 11.4 %collective-permute-start.4 = (f32[80,256]{1,0:T(8,128)S(1)}, f32[80,256]{1,0:T(8,128)S(1)}, u32[]{:S(2)}, u32[]{:S(2)}) collective-permute-start(f32[80,256]{1,0:T(8,128)S(1)} %get-tuple-element.32), channel_id=1, source_target_pairs={{0,4},{4,0},{8,12},{12,8},{16,20},{20,16},{24,28},{28,24},{1,5},{5... | collective-permute-start | bytes 245768 | tf_op jit(solution)/shard_map/ppermute | solution.py:381
  12.0 10.2 %collective-permute-start.5 = (f32[80,256]{1,0:T(8,128)S(1)}, f32[80,256]{1,0:T(8,128)S(1)}, u32[]{:S(2)}, u32[]{:S(2)}) collective-permute-start(f32[80,256]{1,0:T(8,128)S(1)} %get-tuple-element.33), channel_id=1, source_target_pairs={{0,12},{4,8},{8,4},{12,0},{16,28},{20,24},{24,20},{28,16},{1,13},{... | collective-permute-start | bytes 245768 | tf_op jit(solution)/shard_map/ppermute | solution.py:381
  19.0 5.0 %collective-permute-start.6 = (f32[80,256]{1,0:T(8,128)S(1)}, f32[80,256]{1,0:T(8,128)S(1)}, u32[]{:S(2)}, u32[]{:S(2)}) collective-permute-start(f32[80,256]{1,0:T(8,128)S(1)} %get-tuple-element.34), channel_id=1, source_target_pairs={{0,8},{4,12},{8,0},{12,4},{16,24},{20,28},{24,16},{28,20},{1,9},{5... | collective-permute-start | bytes 245768 | tf_op jit(solution)/shard_map/ppermute | solution.py:381
  25.3 3.6 %collective-permute-start.7 = (f32[144,128]{1,0:T(8,128)S(1)}, f32[144,128]{1,0:T(8,128)S(1)}, u32[]{:S(2)}, u32[]{:S(2)}) collective-permute-start(f32[144,128]{1,0:T(8,128)S(1)} %get-tuple-element.37), channel_id=1, source_target_pairs={{0,1},{1,0},{2,3},{3,2},{4,5},{5,4},{6,7},{7,6},{8,9},{9,8},{10,11... | collective-permute-start | bytes 221192 | tf_op jit(solution)/shard_map/ppermute | solution.py:381
  26.3 1.3 %collective-permute-start.12 = (f32[136,128]{1,0:T(8,128)S(1)}, f32[136,128]{1,0:T(8,128)S(1)}, u32[]{:S(2)}, u32[]{:S(2)}) collective-permute-start(f32[136,128]{1,0:T(8,128)S(1)} %get-tuple-element.45), channel_id=1, source_target_pairs={{0,1},{1,0},{2,3},{3,2},{4,5},{5,4},{6,7},{7,6},{8,9},{9,8},{10,11... | collective-permute-start | bytes 208904 | tf_op jit(solution)/shard_map/ppermute | solution.py:381
  27.7 5.0 %collective-permute-start.13 = (f32[256,128]{1,0:T(8,128)S(1)}, f32[256,128]{1,0:T(8,128)S(1)}, u32[]{:S(2)}, u32[]{:S(2)}) collective-permute-start(f32[256,128]{1,0:T(8,128)S(1)} %get-tuple-element.46), channel_id=1, source_target_pairs={{0,2},{1,3},{2,0},{3,1},{4,6},{5,7},{6,4},{7,5},{8,10},{9,11},{10,... | collective-permute-start | bytes 393224 | tf_op jit(solution)/shard_map/ppermute | solution.py:381
  29.1 8.2 %collective-permute-start.8 = (f32[256,128]{1,0:T(8,128)S(1)}, f32[256,128]{1,0:T(8,128)S(1)}, u32[]{:S(2)}, u32[]{:S(2)}) collective-permute-start(f32[256,128]{1,0:T(8,128)S(1)} %get-tuple-element.38), channel_id=1, source_target_pairs={{0,2},{1,3},{2,0},{3,1},{4,6},{5,7},{6,4},{7,5},{8,10},{9,11},{10,... | collective-permute-start | bytes 393224 | tf_op jit(solution)/shard_map/ppermute | solution.py:381
  29.4 2.8 %collective-permute-start.9 = (f32[8,128]{1,0:T(8,128)S(1)}, f32[8,128]{1,0:T(8,128)S(1)}, u32[]{:S(2)}, u32[]{:S(2)}) collective-permute-start(f32[8,128]{1,0:T(8,128)S(1)} %get-tuple-element.40), channel_id=1, source_target_pairs={{0,4},{4,0},{8,12},{12,8},{16,20},{20,16},{24,28},{28,24},{1,5},{5... | collective-permute-start | bytes 12296 | tf_op jit(solution)/shard_map/ppermute | solution.py:381
  32.7 9.2 %collective-permute-start.14 = (f32[136,128]{1,0:T(8,128)S(1)}, f32[136,128]{1,0:T(8,128)S(1)}, u32[]{:S(2)}, u32[]{:S(2)}) collective-permute-start(f32[136,128]{1,0:T(8,128)S(1)} %get-tuple-element.48), channel_id=1, source_target_pairs={{0,8},{1,12},{2,10},{3,14},{4,9},{5,13},{6,11},{7,15},{8,0},{9,4},... | collective-permute-start | bytes 208904 | tf_op jit(solution)/shard_map/ppermute | solution.py:397
  34.8 7.1 %collective-permute-start.15 = (f32[136,128]{1,0:T(8,128)S(1)}, f32[136,128]{1,0:T(8,128)S(1)}, u32[]{:S(2)}, u32[]{:S(2)}) collective-permute-start(f32[136,128]{1,0:T(8,128)S(1)} %get-tuple-element.49), channel_id=1, source_target_pairs={{0,0},{1,4},{2,2},{3,6},{4,1},{5,5},{6,3},{7,7},{8,8},{9,12},{10,1... | collective-permute-start | bytes 208904 | tf_op jit(solution)/shard_map/ppermute | solution.py:397
  37.4 7.4 %collective-permute-start.10 = (f32[136,128]{1,0:T(8,128)S(1)}, f32[136,128]{1,0:T(8,128)S(1)}, u32[]{:S(2)}, u32[]{:S(2)}) collective-permute-start(f32[136,128]{1,0:T(8,128)S(1)} %get-tuple-element.42), channel_id=1, source_target_pairs={{0,16},{1,20},{2,18},{3,22},{4,17},{5,21},{6,19},{7,23},{8,24},{9,... | collective-permute-start | bytes 208904 | tf_op jit(solution)/shard_map/ppermute | solution.py:397
  41.5 6.4 %collective-permute-start.11 = (f32[136,128]{1,0:T(8,128)S(1)}, f32[136,128]{1,0:T(8,128)S(1)}, u32[]{:S(2)}, u32[]{:S(2)}) collective-permute-start(f32[136,128]{1,0:T(8,128)S(1)} %get-tuple-element.43), channel_id=1, source_target_pairs={{0,24},{1,28},{2,26},{3,30},{4,25},{5,29},{6,27},{7,31},{8,16},{9,... | collective-permute-start | bytes 208904 | tf_op jit(solution)/shard_map/ppermute | solution.py:397
